TPU v7x, 32 devices: a 4x2x2 block of a 4x4x8 slice. The times are simulated.
32 devices in a mesh: dp: 4 (over y, z), tp: 8 (over x, core).
Axes of the slice: x: 4, y: 2, z: 2, core: 2. Of those that a mesh axis runs over, the one named last changes fastest.
The devices are a block of a 4x4x8 slice.
Arguments:
- x_in: bfloat16 [4, 3072, 3584], P('dp', 'tp'), parts along dimension 0
- positions: int32 [4, 3072], P('dp', 'tp'), parts along dimension 0
- grad_out: bfloat16 [4, 3072, 3584], P('dp', 'tp'), parts along dimension 0
- w_query: bfloat16 [3584, 16, 256], P(None, 'tp')
- w_key: bfloat16 [3584, 8, 256], P(None, 'tp')
- w_value: bfloat16 [3584, 8, 256], P(None, 'tp')
- w_out: bfloat16 [16, 256, 3584], P('tp')
- gain_pre: float32 [3584], replicated
- gain_post: float32 [3584], replicated
Outputs:
- output 1: bfloat16 [4, 3072, 3584], P('dp', 'tp'), parts along dimension 0
- output 2: bfloat16 [4, 3072, 3584], P('dp', 'tp'), parts along dimension 0
- output 3: float32 [14336, 16, 256], P('dp', 'tp'), parts along dimension 0
- output 4: float32 [14336, 8, 256], P('dp', 'tp'), parts along dimension 0
- output 5: float32 [14336, 8, 256], P('dp', 'tp'), parts along dimension 0
- output 6: float32 [64, 256, 3584], P(('dp', 'tp')), parts along dimension 0
- output 7: float32 [14336], P('dp'), parts along dimension 0
- output 8: float32 [14336], P('dp'), parts along dimension 0
There are 4 independent parts. A program takes and returns all parts, laid end to end along the dimension named above; an argument that names none is the same for every part.
All inputs are finite; a program needn't handle non-finite values.
Results may differ from a plain program's by a relative error of at most 0.0190464.
Values are sent between devices in bfloat16 or wider.
A program may use at most 768 MiB of HBM per device.

v0:
```python
import jax
import jax.numpy as jnp
from jax import lax
from jax.sharding import PartitionSpec as P

WINDOW = 4096
SOFT_CAP = 50.0
NORM_EPS = 1e-6
ROPE_THETA = 10000.0


def rms_norm(hidden, scale_w):
    values = hidden.astype(jnp.float32)
    inv_rms = lax.rsqrt(jnp.mean(values * values, axis=-1, keepdims=True) + NORM_EPS)
    return (values * inv_rms * (1.0 + scale_w)).astype(jnp.bfloat16)


def rope_tables(positions, head_dim):
    half_dim = head_dim // 2
    inv_freq = ROPE_THETA ** (-2.0 * jnp.arange(half_dim, dtype=jnp.float32) / head_dim)
    angles = positions.astype(jnp.float32)[:, :, None] * inv_freq
    return jnp.cos(angles)[:, :, None, :], jnp.sin(angles)[:, :, None, :]


def apply_rope(values, cos_t, sin_t):
    half_dim = values.shape[-1] // 2
    lo_half = values[..., :half_dim]
    hi_half = values[..., half_dim:]
    return jnp.concatenate([lo_half * cos_t - hi_half * sin_t, hi_half * cos_t + lo_half * sin_t], axis=-1)


def rope_transpose(grad_in, cos_t, sin_t):
    half_dim = grad_in.shape[-1] // 2
    lo_half = grad_in[..., :half_dim]
    hi_half = grad_in[..., half_dim:]
    return jnp.concatenate([lo_half * cos_t + hi_half * sin_t, hi_half * cos_t - lo_half * sin_t], axis=-1)


def block_probs(q_blk, k_blk, pos_q, pos_k):
    scores = jnp.einsum('bqkgd,bskd->bkgqs', q_blk, k_blk, preferred_element_type=jnp.float32)
    capped = SOFT_CAP * jnp.tanh(scores / SOFT_CAP)
    pos_gap = pos_q[:, :, None] - pos_k[:, None, :]
    in_window = ((pos_gap >= 0) & (pos_gap < WINDOW))[:, None, None, :, :]
    return capped, jax.nn.softmax(jnp.where(in_window, capped, -1e30), axis=-1)


def attention_fwd(q_all, k_all, v_all, positions):
    seq_len = positions.shape[1]
    q_block = min(128, seq_len)
    slab_len = min(WINDOW + q_block, seq_len)

    def block_step(blk_idx, out_acc):
        q_start = blk_idx * q_block
        k_start = jnp.maximum(q_start + q_block - slab_len, 0)
        q_blk = lax.dynamic_slice_in_dim(q_all, q_start, q_block, axis=1)
        k_blk = lax.dynamic_slice_in_dim(k_all, k_start, slab_len, axis=1)
        v_blk = lax.dynamic_slice_in_dim(v_all, k_start, slab_len, axis=1)
        pos_q = lax.dynamic_slice_in_dim(positions, q_start, q_block, axis=1)
        pos_k = lax.dynamic_slice_in_dim(positions, k_start, slab_len, axis=1)
        prob_blk = block_probs(q_blk, k_blk, pos_q, pos_k)[1]
        out_blk = jnp.einsum('bkgqs,bskd->bqkgd', prob_blk.astype(jnp.bfloat16), v_blk, preferred_element_type=jnp.float32)
        return lax.dynamic_update_slice_in_dim(out_acc, out_blk.astype(jnp.bfloat16), q_start, axis=1)

    return lax.fori_loop(0, seq_len // q_block, block_step, jnp.zeros_like(q_all))


def attention_bwd(q_all, k_all, v_all, positions, d_out):
    seq_len = positions.shape[1]
    q_block = min(128, seq_len)
    slab_len = min(WINDOW + q_block, seq_len)

    def block_step(blk_idx, grad_acc):
        d_q, d_k, d_v = grad_acc
        q_start = blk_idx * q_block
        k_start = jnp.maximum(q_start + q_block - slab_len, 0)
        q_blk = lax.dynamic_slice_in_dim(q_all, q_start, q_block, axis=1)
        k_blk = lax.dynamic_slice_in_dim(k_all, k_start, slab_len, axis=1)
        v_blk = lax.dynamic_slice_in_dim(v_all, k_start, slab_len, axis=1)
        do_blk = lax.dynamic_slice_in_dim(d_out, q_start, q_block, axis=1)
        pos_q = lax.dynamic_slice_in_dim(positions, q_start, q_block, axis=1)
        pos_k = lax.dynamic_slice_in_dim(positions, k_start, slab_len, axis=1)
        capped, prob_blk = block_probs(q_blk, k_blk, pos_q, pos_k)
        d_prob = jnp.einsum('bqkgd,bskd->bkgqs', do_blk, v_blk, preferred_element_type=jnp.float32)
        dv_blk = jnp.einsum('bkgqs,bqkgd->bskd', prob_blk.astype(jnp.bfloat16), do_blk, preferred_element_type=jnp.float32)
        d_capped = prob_blk * (d_prob - jnp.sum(prob_blk * d_prob, axis=-1, keepdims=True))
        d_score = (d_capped * (1.0 - jnp.square(capped / SOFT_CAP))).astype(jnp.bfloat16)
        dq_blk = jnp.einsum('bkgqs,bskd->bqkgd', d_score, k_blk, preferred_element_type=jnp.float32)
        dk_blk = jnp.einsum('bkgqs,bqkgd->bskd', d_score, q_blk, preferred_element_type=jnp.float32)
        d_q = lax.dynamic_update_slice_in_dim(d_q, dq_blk, q_start, axis=1)
        d_k = lax.dynamic_update_slice_in_dim(d_k, lax.dynamic_slice_in_dim(d_k, k_start, slab_len, axis=1) + dk_blk, k_start, axis=1)
        d_v = lax.dynamic_update_slice_in_dim(d_v, lax.dynamic_slice_in_dim(d_v, k_start, slab_len, axis=1) + dv_blk, k_start, axis=1)
        return d_q, d_k, d_v

    zero_init = (jnp.zeros(q_all.shape, jnp.float32), jnp.zeros(k_all.shape, jnp.float32), jnp.zeros(v_all.shape, jnp.float32))
    return lax.fori_loop(0, seq_len // q_block, block_step, zero_init)


def solution(mesh):
    act_spec = P('dp', 'tp', None)
    head_spec = P(None, 'tp', None)
    grad_spec = P('dp', 'tp', None)
    in_specs = (act_spec, P('dp', 'tp'), act_spec, head_spec, head_spec, head_spec, P('tp', None, None), P(None), P(None))
    out_specs = (act_spec, act_spec, grad_spec, grad_spec, grad_spec, P(('dp', 'tp'), None, None), P('dp'), P('dp'))

    def local_step(x_in, positions, grad_out, w_query, w_key, w_value, w_out, gain_pre, gain_post):
        heads_loc, head_dim = w_query.shape[1], w_query.shape[2]
        kv_loc = w_key.shape[1]
        groups = heads_loc // kv_loc
        q_scale = head_dim ** -0.5
        normed, pre_pullback = jax.vjp(rms_norm, x_in, gain_pre)
        normed_all = lax.all_gather(normed, 'tp', axis=1, tiled=True)
        pos_all = lax.all_gather(positions, 'tp', axis=1, tiled=True)
        n_rows, seq_len = pos_all.shape
        cos_t, sin_t = rope_tables(pos_all, head_dim)
        q_lin = jnp.einsum('bsd,dhe->bshe', normed_all, w_query, preferred_element_type=jnp.float32)
        k_lin = jnp.einsum('bsd,dhe->bshe', normed_all, w_key, preferred_element_type=jnp.float32)
        v_lin = jnp.einsum('bsd,dhe->bshe', normed_all, w_value, preferred_element_type=jnp.float32)
        q_all = (apply_rope(q_lin, cos_t, sin_t) * q_scale).astype(jnp.bfloat16).reshape(n_rows, seq_len, kv_loc, groups, head_dim)
        k_all = apply_rope(k_lin, cos_t, sin_t).astype(jnp.bfloat16)
        v_all = v_lin.astype(jnp.bfloat16)
        attn_out = attention_fwd(q_all, k_all, v_all, pos_all).reshape(n_rows, seq_len, heads_loc, head_dim)
        part_proj = jnp.einsum('bshe,hed->bsd', attn_out, w_out, preferred_element_type=jnp.float32)
        proj_loc = lax.psum_scatter(part_proj.astype(jnp.bfloat16), 'tp', scatter_dimension=1, tiled=True)
        post_norm, post_pullback = jax.vjp(rms_norm, proj_loc, gain_post)
        y_out = (x_in.astype(jnp.float32) + post_norm.astype(jnp.float32)).astype(jnp.bfloat16)
        d_proj, d_gain_post = post_pullback(grad_out)
        d_proj_all = lax.all_gather(d_proj, 'tp', axis=1, tiled=True)
        d_attn = jnp.einsum('bsd,hed->bshe', d_proj_all, w_out, preferred_element_type=jnp.float32).astype(jnp.bfloat16)
        grad_wo = jnp.einsum('bshe,bsd->hed', attn_out, d_proj_all, preferred_element_type=jnp.float32)
        d_q, d_k, d_v = attention_bwd(q_all, k_all, v_all, pos_all, d_attn.reshape(n_rows, seq_len, kv_loc, groups, head_dim))
        dq_lin = (rope_transpose(d_q.reshape(n_rows, seq_len, heads_loc, head_dim), cos_t, sin_t) * q_scale).astype(jnp.bfloat16)
        dk_lin = rope_transpose(d_k, cos_t, sin_t).astype(jnp.bfloat16)
        dv_lin = d_v.astype(jnp.bfloat16)
        grad_wq = jnp.einsum('bsd,bshe->dhe', normed_all, dq_lin, preferred_element_type=jnp.float32)
        grad_wk = jnp.einsum('bsd,bshe->dhe', normed_all, dk_lin, preferred_element_type=jnp.float32)
        grad_wv = jnp.einsum('bsd,bshe->dhe', normed_all, dv_lin, preferred_element_type=jnp.float32)
        d_normed = (jnp.einsum('bshe,dhe->bsd', dq_lin, w_query, preferred_element_type=jnp.float32)
                    + jnp.einsum('bshe,dhe->bsd', dk_lin, w_key, preferred_element_type=jnp.float32)
                    + jnp.einsum('bshe,dhe->bsd', dv_lin, w_value, preferred_element_type=jnp.float32))
        d_normed_loc = lax.psum_scatter(d_normed.astype(jnp.bfloat16), 'tp', scatter_dimension=1, tiled=True)
        d_x_norm, d_gain_pre = pre_pullback(d_normed_loc)
        grad_x = (grad_out.astype(jnp.float32) + d_x_norm.astype(jnp.float32)).astype(jnp.bfloat16)
        grad_pre = lax.psum(d_gain_pre, 'tp')
        grad_post = lax.psum(d_gain_post, 'tp')
        return y_out, grad_x, grad_wq, grad_wk, grad_wv, grad_wo, grad_pre, grad_post

    return jax.shard_map(local_step, mesh=mesh, in_specs=in_specs, out_specs=out_specs, check_vma=False)
```

profile of v0, /device:TPU:88, one launch (start us, length us, event | category | flops | bytes accessed | tf_op | source)
XLA Modules:
  0.0 1416.0 jit_solution(13758626951535086585)
XLA Ops:
  14.3 13.4 all_gather.9
  27.8 6.8 multiply_cosine_fusion.1
  34.6 86.9 %all-gather.3.cloned.1.call-done = bf16[1,3072,3584]{2,1,0:T(8,128)(2,1)} async-done(((bf16[1,384,3584]{2,1,0:T(8,128)(2,1)}), bf16[1,3072,3584]{2,1,0:T(8,128)(2,1)}) %all-gather.3.cloned.1.call-update) | async-done | bytes 22020112 | tf_op jit(solution)/shard_map/all_gather | solution.py:111
  121.5 12.0 fusion.113
  133.4 8.2 fusion.144
  145.5 19.2 %fusion.107 = f32[1,3072,2,256]{1,3,2,0:T(8,128)} fusion(bf16[1,3072,3584]{2,1,0:T(8,128)(2,1)} %all-gather.3.cloned.1.call-done, bf16[3584,2,256]{2,1,0:T(2,128)(2,1)} %param.16), kind=kOutput, calls=%fused_computation.126 | convolution fusion | flops 11274289152 | bytes 31981568 | tf_op jit(solution)/shard_map/bsd,dhe->bshe/dot_general | solution.py:115
  171.4 4.6 copy.20
  176.1 11.6 fusion.122
  189.5 154.3 %while.33 = (s32[]{:T(128)}, bf16[1,3072,1,2,256]{4,1,3,2,0:T(8,128)(2,1)}, s32[1,3072]{1,0:T(1,128)S(1)}, bf16[1,3072,1,2,256]{4,1,3,2,0:T(8,128)(2,1)}, bf16[1...) while((s32[]{:T(128)}, ...), condition=%wide.region_4.5_spmd, body=%wide.region_1.4_spmd.sunk | while | flops 814022144 | bytes 13650591 | solution.py:64
  343.9 18.5 %fusion.82 = bf16[1,3072,3584]{2,1,0:T(8,128)(2,1)} fusion(bf16[2,256,3584]{2,1,0:T(8,128)(2,1)} %param.19, bf16[1,3072,1,2,256]{4,1,3,2,0:T(8,128)(2,1)} %get-tuple-element.339), kind=kOutput, calls=%fused_computation.87 | convolution fusion | flops 11285299200 | bytes 28835840 | tf_op jit(solution)/shard_map/bshe,hed->bsd/dot_general | solution.py:122
  363.1 113.7 %reduce-scatter.3.cloned.1.call-done = bf16[1,384,3584]{2,1,0:T(8,128)(2,1)} async-done(((bf16[1,3072,3584]{2,1,0:T(8,128)(2,1)}), bf16[1,384,3584]{2,1,0:T(8,128)(2,1)}) %reduce-scatter.3.cloned.1.call-update) | async-done | bytes 2752528 | tf_op jit(solution)/shard_map/reduce_scatter | solution.py:123
  479.4 5.8 fusion.93
  489.6 104.1 %all-gather.5.cloned.1.call-done = bf16[1,3072,3584]{2,1,0:T(8,128)(2,1)} async-done(((bf16[1,384,3584]{2,1,0:T(8,128)(2,1)}), bf16[1,3072,3584]{2,1,0:T(8,128)(2,1)}) %all-gather.5.cloned.1.call-update) | async-done | bytes 22020112 | tf_op jit(solution)/shard_map/all_gather | solution.py:127
  593.6 18.4 %fusion.116 = bf16[1,3072,1,2,256]{4,1,3,2,0:T(8,128)(2,1)} fusion(bf16[2,256,3584]{2,1,0:T(8,128)(2,1)} %param.19, bf16[1,3072,3584]{2,1,0:T(8,128)(2,1)} %all-gather.5.cloned.1.call-done), kind=kOutput, calls=%fused_computation.129 | convolution fusion | flops 11275862016 | bytes 28835840 | tf_op jit(solution)/shard_map/bsd,hed->bshe/dot_general | solution.py:128
  615.5 549.8 %while.34 = (s32[]{:T(128)}, f32[1,3072,1,2,256]{1,4,3,2,0:T(8,128)}, f32[1,3072,1,256]{1,3,2,0:T(8,128)}, f32[1,3072,1,256]{1,3,2,0:T(8,128)}, s32[1,3072]{1,0:...) while((s32[]{:T(128)}, ...), condition=%wide.region_12.0_spmd.clone, body=%wide.region_8.12_spmd.clone.sunk | while | flops 2040790272 | bytes 49308400 | solution.py:95
  640.3 5.1 fusion.216
  654.3 4.3 fusion.215
  663.3 5.1 fusion.216
  686.2 5.1 fusion.216
  700.3 4.3 fusion.215
  709.2 5.1 fusion.216
  723.3 4.3 fusion.215
  732.2 5.1 fusion.216
  755.2 5.1 fusion.216
  769.2 4.3 fusion.215
  778.2 5.1 fusion.216
  792.2 4.3 fusion.215
  801.1 5.1 fusion.216
  815.2 4.3 fusion.215
  824.1 5.1 fusion.216
  838.2 4.3 fusion.215
  847.1 5.1 fusion.216
  870.1 5.1 fusion.216
  884.1 4.3 fusion.215
  893.1 5.1 fusion.216
  907.1 4.3 fusion.215
  916.1 5.1 fusion.216
  939.0 5.1 fusion.216
  953.1 4.3 fusion.215
  962.0 5.1 fusion.216
  985.0 5.1 fusion.216
  1008.0 5.1 fusion.216
  1031.0 5.1 fusion.216
  1053.9 5.1 fusion.216
  1076.9 5.1 fusion.216
  1099.9 5.1 fusion.216
  1122.9 5.1 fusion.216
  1145.9 5.1 fusion.216
  1165.3 8.1 add_bitcast_fusion
  1173.5 6.1 fusion.156
  1179.6 19.0 %fusion.137 = f32[3072,3584]{1,0:T(8,128)} fusion(bf16[3584,1,256]{2,0,1:T(8,128)(2,1)S(1)} %copy-done, f32[1,3072,1,256]{1,3,2,0:T(8,128)} %get-tuple-element.342), kind=kOutput, calls=%fused_computation.152 | convolution fusion | flops 5637931008 | bytes 49020928 | tf_op jit(solution)/shard_map/bshe,dhe->bsd/dot_general | solution.py:139
  1198.6 18.5 %fusion.140 = f32[3072,3584]{1,0:T(8,128)} fusion(bf16[3584,1,256]{2,0,1:T(8,128)(2,1)} %param.17, bf16[3072,128]{0,1:T(8,128)(2,1)S(1)} %get-tuple-element.443, bf16[3072,128]{0,1:T(8,128)(2,1)S(1)} %get-tuple-element.442), kind=kOutput, calls=%fused_computation.155 | convolution fusion | flops 5640290304 | bytes 47448064 | tf_op jit(solution)/shard_map/bshe,dhe->bsd/dot_general | solution.py:138
  1217.1 39.6 %fusion.81 = bf16[1,3072,3584]{2,1,0:T(8,128)(2,1)} fusion(f32[3072,3584]{1,0:T(8,128)} %fusion.137, f32[3072,3584]{1,0:T(8,128)} %fusion.140, bf16[3584,2,256]{2,1,0:T(2,128)(2,1)} %param.16, f32[3072,2,128]{0,2,1:T(8,128)} %get-tuple-element.439, f32[3072,2,128]{0,2,1:T(8,128)} %get-tuple-element.438), kind=kOutput, calls=%fused_computation.86 | convolution fusion | flops 11312037888 | bytes 120061952 | tf_op jit(solution)/shard_map/bshe,dhe->bsd/dot_general | solution.py:137
  1256.7 10.8 fusion.104
  1267.6 16.9 %copy.31 = f32[3584,1,256]{2,1,0:T(1,128)} copy(f32[3584,1,256]{2,0,1:T(8,128)S(1)} %fusion.104) | data formatting | bytes 7340032
  1284.5 18.1 %fusion.69 = f32[3584,2,256]{2,0,1:T(8,128)} fusion(bf16[1,3072,3584]{2,1,0:T(8,128)(2,1)} %all-gather.3.cloned.1.call-done, f32[3072,2,128]{0,2,1:T(8,128)S(1)} %copy-done.9, f32[3072,2,128]{0,2,1:T(8,128)S(1)} %copy-done.8), kind=kOutput, calls=%fused_computation.74 | convolution fusion | flops 11279007744 | bytes 35651584 | tf_op jit(solution)/shard_map/bsd,bshe->dhe/dot_general | solution.py:134
  1302.6 13.9 copy.30
  1316.5 11.6 fusion.101
  1328.1 16.9 %copy.32 = f32[3584,1,256]{2,1,0:T(1,128)} copy(f32[3584,1,256]{2,0,1:T(8,128)S(1)} %fusion.101) | data formatting | bytes 7340032
  1344.9 18.3 %fusion.65 = f32[2,256,3584]{2,1,0:T(8,128)} fusion(bf16[1,3072,3584]{2,1,0:T(8,128)(2,1)} %all-gather.5.cloned.1.call-done, bf16[1,3072,1,2,256]{4,1,3,2,0:T(8,128)(2,1)S(1)} %copy-done.10), kind=kOutput, calls=%fused_computation.70 | convolution fusion | flops 11274289152 | bytes 32505856 | tf_op jit(solution)/shard_map/bshe,bsd->hed/dot_general | solution.py:129
  1363.2 8.5 reduce-scatter.5.cloned.1.call-done
  1371.7 5.9 fusion.91
  1377.7 24.5 %all-reduce = (f32[3584]{0:T(1024)}, f32[3584]{0:T(1024)}) all-reduce(f32[3584]{0:T(1024)S(1)} %get-tuple-element.398, f32[3584]{0:T(1024)S(1)} %copy-done.15), channel_id=1, replica_groups=mesh['dp'=4,'tp'=8] {'tp'}, use_global_device_ids=true, to_apply=%region_16.17 | all-reduce | flops 7168 | bytes 57344 | tf_op jit(solution)/shard_map/psum | solution.py:143
  1402.2 7.0 fusion.92
  (473 shorter events, 572.6 us)
Async XLA Ops:
  7.2 168.9 %copy-start = (bf16[3584,1,256]{2,0,1:T(8,128)(2,1)S(1)}, bf16[3584,1,256]{2,0,1:T(8,128)(2,1)}, u32[]{:S(2)}) copy-start(bf16[3584,1,256]{2,0,1:T(8,128)(2,1)} %param.18) | copy-start | bytes 5505028
  7.2 114.3 %all-gather.3.cloned.1.call-start = ((), (), s32[]{:S(2)}) async-start(), calls=%async_computation.2 | async-start | bytes 24772608 | tf_op jit(solution)/shard_map/all_gather | solution.py:111
  7.3 4.5 copy-start.2
  9.8 0.6 copy-start.18
  10.4 0.7 copy-start.16
  11.2 0.6 copy-start.11
  11.8 2.5 copy-start.23
  14.2 462.6 %reduce-scatter.3.cloned.1.call-start = ((), (), s32[]{:S(2)}) async-start(), calls=%async_computation.3 | async-start | bytes 24772608 | tf_op jit(solution)/shard_map/reduce_scatter | solution.py:123
  27.7 105.7 %copy-start.13 = (f32[1,3072]{1,0:T(1,128)}, f32[1,3072]{1,0:T(1,128)S(1)}, u32[]{:S(2)}) copy-start(f32[1,3072]{1,0:T(1,128)S(1)} %convert_element_type.144) | copy-start | bytes 36868
  27.7 105.7 %copy-start.21 = (f32[128]{0:T(128)}, f32[128]{0:T(128)S(1)}, u32[]{:S(2)}) copy-start(f32[128]{0:T(128)S(1)} %multiply_power_fusion) | copy-start | bytes 1540
  34.6 130.2 %copy-start.7 = (f32[3072,128]{0,1:T(8,128)}, f32[3072,128]{0,1:T(8,128)S(1)}, u32[]{:S(2)}) copy-start(f32[3072,128]{0,1:T(8,128)S(1)} %get-tuple-element.448) | copy-start | bytes 4718596
  362.3 0.7 copy-start.20
  362.4 231.2 %all-gather.5.cloned.1.call-start = ((), (), s32[]{:S(2)}) async-start(), calls=%async_computation.4 | async-start | bytes 24772608 | tf_op jit(solution)/shard_map/all_gather | solution.py:127
  476.8 2.6 copy-start.5
  479.3 5.9 copy-start.3
  479.3 5.9 copy-start.6
  489.5 882.2 %reduce-scatter.5.cloned.1.call-start = ((), (), s32[]{:S(2)}) async-start(), calls=%async_computation.5 | async-start | bytes 24772608 | tf_op jit(solution)/shard_map/reduce_scatter | solution.py:140
  632.4 3.2 copy-start.4
  654.3 4.3 copy-start.4
  677.3 4.3 copy-start.4
  700.3 4.3 copy-start.4
  723.3 4.3 copy-start.4
  746.3 4.3 copy-start.4
  769.2 4.3 copy-start.4
  792.2 4.3 copy-start.4
  815.2 4.3 copy-start.4
  838.2 4.3 copy-start.4
  861.2 4.3 copy-start.4
  884.1 4.3 copy-start.4
  907.1 4.3 copy-start.4
  930.1 4.3 copy-start.4
  953.1 4.3 copy-start.4
  976.1 4.3 copy-start.4
  999.0 4.3 copy-start.4
  1022.0 4.3 copy-start.4
  1045.0 4.3 copy-start.4
  1068.0 4.3 copy-start.4
  1091.0 4.3 copy-start.4
  1113.9 4.3 copy-start.4
  1136.9 4.3 copy-start.4
  1159.9 4.3 copy-start.4
  1165.3 8.2 copy-start.1
  1165.3 8.2 copy-start.14
  1165.3 8.1 copy-start.22
  1267.6 16.9 %copy-start.8 = (f32[3072,2,128]{0,2,1:T(8,128)S(1)}, f32[3072,2,128]{0,2,1:T(8,128)}, u32[]{:S(2)}) copy-start(f32[3072,2,128]{0,2,1:T(8,128)} %get-tuple-element.438) | copy-start | bytes 9437188
  1267.6 16.9 %copy-start.9 = (f32[3072,2,128]{0,2,1:T(8,128)S(1)}, f32[3072,2,128]{0,2,1:T(8,128)}, u32[]{:S(2)}) copy-start(f32[3072,2,128]{0,2,1:T(8,128)} %get-tuple-element.439) | copy-start | bytes 9437188
  1328.1 16.9 %copy-start.10 = (bf16[1,3072,1,2,256]{4,1,3,2,0:T(8,128)(2,1)S(1)}, bf16[1,3072,1,2,256]{4,1,3,2,0:T(8,128)(2,1)}, u32[]{:S(2)}) copy-start(bf16[1,3072,1,2,256]{4,1,3,2,0:T(8,128)(2,1)} %get-tuple-element.339) | copy-start | bytes 9437188
  1344.9 26.7 %copy-start.12 = (f32[3584]{0:T(1024)S(1)}, f32[3584]{0:T(1024)}, u32[]{:S(2)}) copy-start(f32[3584]{0:T(1024)} %copy-done.11) | copy-start | bytes 43012
  1344.9 26.7 %copy-start.17 = (f32[384]{0:T(512)S(1)}, f32[384]{0:T(512)}, u32[]{:S(2)}) copy-start(f32[384]{0:T(512)} %copy-done.16) | copy-start | bytes 4612
  1363.2 14.4 %copy-start.19 = (f32[384]{0:T(512)S(1)}, f32[384]{0:T(512)}, u32[]{:S(2)}) copy-start(f32[384]{0:T(512)} %copy-done.18) | copy-start | bytes 4612
  1363.2 14.4 %copy-start.15 = (f32[3584]{0:T(1024)S(1)}, f32[3584]{0:T(1024)}, u32[]{:S(2)}) copy-start(f32[3584]{0:T(1024)} %get-tuple-element.396) | copy-start | bytes 43012
Sparse Core Ops, SparseCore 0:
  14.3 107.0 all-gather.2
  362.5 114.2 reduce-scatter.2
  489.6 103.9 all-gather.4
  1256.9 114.7 reduce-scatter.4
where the time goes:
time: 1420 us
  matrix products  767 us (54%)
  waiting for transfers between devices  313 us (22%)
  other arithmetic  160 us (11%)
  local copies, waits for them, and re-layouts  123 us (9%)
  blocking collectives  38 us (3%)
  between operations  14.3 us (1%)
    dot_general x48, matrix products, block_probs(): jnp.einsum('bqkgd,bskd->bkgqs', q_blk, k_blk, preferred_element_type=jnp....  126 us
    dot_general x24, matrix products, block_step(): jnp.einsum('bkgqs,bqkgd->bskd', prob_blk.astype(jnp.bfloat16), do_blk, pr...  122 us
    reduce_scatter x1, waiting for transfers between devices, local_step(): lax.psum_scatter(part_proj.astype(jnp.bfloat16), 'tp', scatter_dimension=...  114 us
    all_gather x1, waiting for transfers between devices, local_step(): d_proj_all = lax.all_gather(d_proj, 'tp', axis=1, tiled=True)  104 us
    dot_general x24, matrix products, block_step(): jnp.einsum('bkgqs,bqkgd->bskd', d_score, q_blk, preferred_element_type=jn...  102 us
    all_gather x1, waiting for transfers between devices, local_step(): normed_all = lax.all_gather(normed, 'tp', axis=1, tiled=True)  86.9 us
    dot_general x24, matrix products, block_step(): jnp.einsum('bqkgd,bskd->bkgqs', do_blk, v_blk, preferred_element_type=jnp...  69.7 us
    dot_general x24, matrix products, block_step(): jnp.einsum('bkgqs,bskd->bqkgd', prob_blk.astype(jnp.bfloat16), v_blk, pre...  67.4 us
  transfers between devices with their start and end apart: 4, of which 4 were waited for; matrix products, arithmetic and copies ran while one was open for 8% of the time, Pallas kernels for 0%

commit v1 on v0

v1 whole, which is shorter than its diff:
```python
import functools

import jax
import jax.numpy as jnp
import numpy as np
from jax import lax
from jax.experimental import pallas as pl
from jax.experimental.pallas import tpu as pltpu
from jax.sharding import PartitionSpec as P


WINDOW = 4096
SOFT_CAP = 50.0
NORM_EPS = 1e-6
ROPE_THETA = 10000.0
LOG2E = 1.4426950408889634
BLK = 128
PIECE = 64
SUB = 16
KT = 512
NBLK = 3
NPC = 6
HALF_PC = 3
CHIPS = 4
DEVS = 8
ALL_BLK = DEVS * NBLK
MY_BLK = CHIPS * NBLK
HD = 256
HD2 = 128
QW = 512
QKV = 1024
ONE, TWO = 1, 2
VMEM_BYTES = 67 * 1000 * 1000
F32 = jnp.float32
BF16 = jnp.bfloat16
I32 = jnp.int32


def dot(a, b):
    return lax.dot_general(a, b, (((1,), (0,)), ((), ())), preferred_element_type=F32)


def dot_bt(a, b):
    return lax.dot_general(a, b, (((1,), (1,)), ((), ())), preferred_element_type=F32)


def dot_at(a, b):
    return lax.dot_general(a, b, (((0,), (0,)), ((), ())), preferred_element_type=F32)


def pick(s, values):
    out = I32(values[0])
    for i, value in enumerate(values):
        if value != values[0]:
            out = jnp.where(s == i, I32(value), out)
    return out


def rcopy(src, dst, ss, rs, dev):
    return pltpu.make_async_remote_copy(src_ref=src, dst_ref=dst, send_sem=ss, recv_sem=rs,
                                        device_id={'tp': dev}, device_id_type=pl.DeviceIdType.MESH)


class Place:
    def __init__(self):
        me = lax.axis_index('tp')
        self.me = me
        self.chip = lax.div(me, TWO)
        self.core = lax.rem(me, TWO)
        self.right = self.dev(ONE, 0)
        self.left = self.dev(CHIPS - ONE, 0)
        self.partner = self.dev(0, ONE)

    def dev(self, chip_off, flip):
        chip = lax.rem(self.chip + chip_off, CHIPS)
        return TWO * chip + lax.rem(self.core + flip, TWO)

    def peers(self):
        return [lax.rem(self.me + d, DEVS) for d in range(ONE, DEVS)]


def barrier(devs):
    sem = pltpu.get_barrier_semaphore()
    for dev in devs:
        pl.semaphore_signal(sem, inc=ONE, device_id={'tp': dev}, device_id_type=pl.DeviceIdType.MESH)
    pl.semaphore_wait(sem, len(devs))


def rows16(r):
    return pl.ds(SUB * r, SUB)


def digits(text):
    return [int(c) for c in text]


AG_OFF = (digits('003033322332'), digits('001011122112'))
AG_FLIP = (digits('000110101010'), digits('010110101011'))
AG_BLK = (digits('020101100221'), digits('102221122001'))
AG_STEPS = len(AG_OFF[0])
AG_FORWARD = {2: ('01', '54'), 5: ('2', '3')}
AG_FIRST = ('0123', '5432')
AG_THEN = ('45', '10')
AG_MADE = digits('051432')
AG_THEN_STEP = 2


def ag_scratch(width):
    dma = pltpu.SemaphoreType.DMA
    return [pltpu.VMEM((ALL_BLK, BLK, width), BF16),
            dma((CHIPS, NPC)),
            dma((CHIPS, NBLK)),
            dma((TWO, NPC)),
            dma((NPC,)),
            dma((CHIPS, NBLK))]


def half_of(i):
    return pl.ds(PIECE * (i % TWO), PIECE)


def piece_of(full, shard, i):
    return full.at[shard * NBLK + i // TWO, half_of(i), :]


def ag_send(p, way, i, src, full, ring_rs, part_rs, own_ss, fwd_ss, part_ss):
    rcopy(src, piece_of(full, p.me, i), own_ss.at[way, i], ring_rs.at[p.chip, i], (p.right, p.left)[way]).start()


def ag_then(s, src):
    @pl.when(s == AG_THEN_STEP)
    def _():
        for way, pieces in enumerate(AG_THEN):
            for i in digits(pieces):
                src(way, i)


def ag_swap(p, chip, blk, src, dst, full, ring_rs, part_rs, own_ss, fwd_ss, part_ss):
    return rcopy(src, dst, part_ss.at[chip, blk], part_rs.at[chip, blk], p.partner)


def ag_block(p, s, n):
    off, flip, blk = pick(s, AG_OFF[n]), pick(s, AG_FLIP[n]), pick(s, AG_BLK[n])
    chip = lax.rem(p.chip + off, CHIPS)
    shard = TWO * chip + lax.rem(p.core + flip, TWO)
    return off, flip, chip, shard, blk, shard * NBLK + blk


def ag_step(p, s, n, full, ring_rs, part_rs, own_ss, fwd_ss, part_ss):
    off, flip, chip, shard, blk, g = ag_block(p, s, n)
    swap = rcopy(full.at[g], full.at[g], part_ss.at[chip, blk], part_rs.at[chip, blk], p.partner)

    @pl.when(flip != 0)
    def _():
        swap.wait_recv()

    @pl.when(jnp.logical_and(flip == 0, off != 0))
    def _():
        for h in range(TWO):
            half = full.at[g, half_of(h), :]
            rcopy(half, half, fwd_ss.at[0], ring_rs.at[chip, TWO * blk + h], p.partner).wait_recv()
        swap.start()

    for step, pieces in AG_FORWARD.items():
        @pl.when(s == step)
        def _(pieces=pieces[n]):
            for i in digits(pieces):
                ref = piece_of(full, shard, i)
                rcopy(ref, ref, fwd_ss.at[i], ring_rs.at[chip, i], (p.right, p.left)[n]).start()
    return g


def ag_finish(p, full, ring_rs, part_rs, own_ss, fwd_ss, part_ss):
    for n in range(NPC):
        ref = piece_of(full, p.me, n)
        for sem in (own_ss.at[0, n], own_ss.at[ONE, n], fwd_ss.at[n]):
            rcopy(ref, ref, sem, ring_rs.at[p.chip, n], p.right).wait_send()
    for c in range(CHIPS):
        for b in range(NBLK):
            ref = full.at[b]
            rcopy(ref, ref, part_ss.at[c, b], part_rs.at[c, b], p.partner).wait_send()


RS_PLAN = ['O23', 'O01', 'O54', 'R54', 'L01', 'X01', 'X23', 'X45', 'R01', 'L54', 'R32', 'L23']


def plan_tables(plan):
    return ([{'O': TWO, 'R': ONE, 'L': CHIPS - ONE, 'X': 0}[step[0]] for step in plan],
            [int(step[ONE]) // TWO for step in plan])


RS_OFF, RS_BLK = plan_tables(RS_PLAN)
RS_STEPS = len(RS_PLAN)
RS_DONE = digits('021')


def rs_scratch(width):
    dma = pltpu.SemaphoreType.DMA
    return [pltpu.VMEM((HALF_PC, NPC, PIECE, width), BF16),
            pltpu.VMEM((HALF_PC, PIECE, width), BF16),
            pltpu.VMEM((HALF_PC, PIECE, width), BF16),
            pltpu.VMEM((TWO, NPC, PIECE, width), BF16),
            pltpu.VMEM((NBLK, BLK, width), BF16),
            dma((HALF_PC, NPC)), dma((HALF_PC,)), dma((HALF_PC,)), dma((TWO, NPC))]


def put_rows(part, dst, i, extra=None):
    @pl.loop(0, PIECE // SUB)
    def _(r):
        v = part[pl.ds(PIECE * (i % TWO) + SUB * r, SUB), :]
        if extra is not None:
            v = v + extra[rows16(r), :].astype(F32)
        dst[rows16(r), :] = v.astype(BF16)


def rs_emit(p, s, part, sent, hop_l, hop_r, fin, own, ss, hl_rs, hr_rs, fin_rs):
    put = functools.partial(put_rows, part)
    for step in range(RS_STEPS):
        kind, pieces, blk = RS_PLAN[step][0], digits(RS_PLAN[step][ONE:]), RS_BLK[step]

        @pl.when(s == step)
        def _(kind=kind, pieces=pieces, blk=blk):
            for i in pieces:
                low, j = i < HALF_PC, i % HALF_PC
                if kind == 'X':
                    put(own.at[blk, half_of(i), :], i)
                    continue
                slot = 'ORL'.index(kind)
                dst = sent.at[slot, i]
                if kind == 'O':
                    put(dst, i)
                    hop, hop_rs, dev = (hop_l, hl_rs, p.right) if low else (hop_r, hr_rs, p.left)
                    rcopy(dst, hop.at[j], ss.at[slot, i], hop_rs.at[j], dev).start()
                    continue
                hop, hop_rs, dev, side = (hop_l, hl_rs, p.right, 0) if kind == 'R' else (hop_r, hr_rs, p.left, ONE)
                if low == (kind == 'R'):
                    rcopy(hop.at[j], hop.at[j], ss.at[slot, i], hop_rs.at[j], dev).wait_recv()
                    put(dst, i, hop.at[j])
                else:
                    put(dst, i)
                rcopy(dst, fin.at[side, i], ss.at[slot, i], fin_rs.at[side, i], dev).start()


def rs_wait_block(p, blk, sent, hop_l, hop_r, fin, own, ss, hl_rs, hr_rs, fin_rs):
    for side in range(TWO):
        for h in range(TWO):
            i = TWO * blk + h
            rcopy(fin.at[side, i], fin.at[side, i], ss.at[0, i], fin_rs.at[side, i], p.right).wait_recv()


def rs_total(blk, r, cols, fin, own):
    per = PIECE // SUB
    i, rows = TWO * blk + lax.div(r, per), rows16(lax.rem(r, per))
    total = (own[blk, rows16(r), cols].astype(F32) + fin[0, i, rows, cols].astype(F32)
             + fin[ONE, i, rows, cols].astype(F32))
    return total.astype(BF16).astype(F32)


def column_groups(width):
    return [pl.ds(QW * c, QW) for c in range(width // QW)]


def fold(val):
    out = val[:, :HD2]
    for c in range(ONE, QW // HD2):
        out = out + val[:, HD2 * c:HD2 * c + HD2]
    return out


def row_mean(parts, width):
    total = parts[0]
    for part in parts[ONE:]:
        total = total + part
    return jnp.sum(total, axis=1, keepdims=True) * (1.0 / width)


def rs_finish(p, sent, hop_l, hop_r, fin, own, ss, hl_rs, hr_rs, fin_rs):
    for slot in range(HALF_PC):
        for i in range(NPC):
            rcopy(sent.at[slot, i], sent.at[slot, i], ss.at[slot, i], fin_rs.at[0, i], p.right).wait_send()


def rope(lin, cos_t, sin_t):
    lo, hi = lin[:, :HD2], lin[:, HD2:]
    return jnp.concatenate([lo * cos_t - hi * sin_t, hi * cos_t + lo * sin_t], axis=1)


def rope_back(grad, cos_t, sin_t):
    lo, hi = grad[:, :HD2], grad[:, HD2:]
    return jnp.concatenate([lo * cos_t + hi * sin_t, hi * cos_t - lo * sin_t], axis=1)


def twice(row):
    return jnp.concatenate([row, row], axis=1)


def heads_down(row_pair):
    return jnp.concatenate([row_pair[:, :HD], row_pair[:, HD:]], axis=0)


def key_mask(pos_q, pos_k):
    gap = twice(pos_q) - twice(pos_k)
    return gap.astype(jnp.uint32) < jnp.uint32(WINDOW)


def head(n):
    return pl.ds(HD * n, HD)


def lanes_at(i, size):
    return pl.ds(pl.multiple_of(i * size, size), size)


def tiles_of(g):
    return lax.div(g * BLK, KT) + ONE


class Walk:
    def __init__(self, ga, gb):
        self.ga, self.gb = ga, gb
        self.na = tiles_of(ga)
        self.n = self.na + tiles_of(gb)
        self.turns = lax.div(self.n + ONE, TWO)

    def pos_q(self, i, pos_row):
        return jnp.where(i < self.n, pos_row, I32(-ONE))

    def at(self, i):
        i = jnp.minimum(jnp.maximum(i, 0), self.n - ONE)
        second = i >= self.na
        return (jnp.where(second, I32(ONE), I32(0)), jnp.where(second, self.gb, self.ga),
                jnp.where(second, i - self.na, i))


def store_columns(full, out, g, sem):
    for c in range(out.shape[0]):
        pltpu.make_async_copy(full.at[g, :, head(c)], out.at[c, g], sem).start()


class Loads:
    def __init__(self, sem):
        self.sem, self.count = sem, 0

    def add(self, src, dst):
        copy = pltpu.make_async_copy(src, dst, self.sem.at[self.count])
        copy.start()
        self.count += ONE
        return copy


def wait_all(copies):
    for copy in copies:
        copy.wait()


def gather_qkv_kernel(q_scale, x, pos_in, inv_freq, gain, wq, wk, wv, wo,
                      nall, q_out, k_out, v_out, kt_out, vt_out, cos_out, sin_out, posb_out, posr_out, wt_out, wtp_out,
                      wop_out, *scratch):
    n_ag = len(ag_scratch(BLK))
    ag, rest = scratch[:n_ag], scratch[n_ag:]
    (x_s, gain_s, wq_s, w_s, wt_s, q_s, k_s, v_s, kt_s, vt_s, cos_s, sin_s, posb_s, pos_s, lsem, osem, wsem, wo_sem, pos_ss,
     pos_rs, nall_sem) = rest
    full = ag[0]
    p = Place()
    loads = Loads(lsem)
    own = [loads.add(gain, gain_s.at[0])]
    own += [loads.add(x.at[i // TWO, half_of(i)], x_s.at[i // TWO, half_of(i)]) for i in AG_MADE]
    barrier(p.peers())

    def pos_copy(n, dev, owner):
        return rcopy(pos_in, pos_s.at[pl.ds(owner * NBLK, NBLK)], pos_ss.at[n], pos_rs.at[owner], dev)

    for n, dev in enumerate(p.peers()):
        pos_copy(n, dev, p.me).start()
    for b in range(NBLK):
        pos_s[p.me * NBLK + b] = pos_in[b]
    own[0].wait()
    for n, i in enumerate(AG_MADE):
        own[n + ONE].wait()
        if n == TWO:
            weights = [loads.add(wq, wq_s), loads.add(wk, w_s.at[:, pl.ds(QW, HD)]),
                       loads.add(wv, w_s.at[:, pl.ds(QW + HD, HD)])]
        b = i // TWO
        g = p.me * NBLK + b

        @pl.loop(0, PIECE // SUB)
        def _(r, b=b, g=g, start=PIECE * (i % TWO)):
            rows = pl.ds(start + SUB * r, SUB)
            val = x_s[b, rows, :].astype(F32)
            inv = lax.rsqrt(jnp.mean(val * val, axis=1, keepdims=True) + NORM_EPS)
            full[g, rows, :] = (val * inv * (1.0 + gain_s[...])).astype(BF16)

        for way, pieces in enumerate(AG_FIRST):
            if i in digits(pieces):
                ag_send(p, way, i, piece_of(full, p.me, i), *ag)
        if i in AG_MADE[TWO:CHIPS] + AG_MADE[-ONE:]:
            ag_swap(p, p.chip, b, full.at[g], full.at[g], *ag).start()
    wo_copy = rcopy(wo, wop_out, wo_sem.at[0], wo_sem.at[ONE], p.partner)
    wo_copy.start()
    for n, dev in enumerate(p.peers()):
        pos_copy(n, dev, dev).wait_recv()
    wait_all(weights)

    @pl.loop(0, w_s.shape[0] // BLK)
    def _(r):
        rows = lanes_at(r, BLK)
        both = wq_s[rows]
        for h in range(TWO):
            w_s[rows, head(h)] = both[:, h, :]

    def out_copies(g):
        tile, lanes = lax.div(g * BLK, KT), lanes_at(lax.rem(g, KT // BLK), BLK)
        return [(q_s.at[:, g], q_out.at[:, g]), (k_s.at[g], k_out.at[g]),
                (v_s.at[g], v_out.at[g]), (cos_s.at[g], cos_out.at[g]), (sin_s.at[g], sin_out.at[g]),
                (posb_s.at[g], posb_out.at[g]), (kt_s.at[tile, :, lanes], kt_out.at[tile, :, lanes]),
                (vt_s.at[tile, :, lanes], vt_out.at[tile, :, lanes])]

    whole = [(q_s, q_out), (k_s, k_out), (v_s, v_out), (cos_s, cos_out), (sin_s, sin_out),
             (posb_s, posb_out), (kt_s, kt_out), (vt_s, vt_out)]

    @pl.loop(0, AG_STEPS)
    def _(s):
        for n in range(TWO):
            g = ag_block(p, s, n)[-ONE]
            pos_row = pos_s[g]
            pos_b = jnp.broadcast_to(pos_row, (BLK, BLK)).T
            posr_out[g] = pos_row
            posb_s[g] = pos_b
            angle = pos_b.astype(F32) * inv_freq[...]
            cos_s[g] = jnp.cos(angle)
            sin_s[g] = jnp.sin(angle)
        pair = [ag_step(p, s, n, *ag) for n in range(TWO)]
        ag_then(s, lambda way, i: ag_send(p, way, i, piece_of(full, p.me, i), *ag))
        rows = jnp.concatenate([full[g] for g in pair], axis=0)
        for part in range(QKV // HD):
            lin = dot(rows, w_s[:, head(part)])
            for n, g in enumerate(pair):
                val = lin[BLK * n:BLK * n + BLK]
                tile, lanes = lax.div(g * BLK, KT), lanes_at(lax.rem(g, KT // BLK), BLK)
                if part < QW // HD:
                    q_s[part, g] = (rope(val, cos_s[g], sin_s[g]) * q_scale).astype(BF16)
                elif part == QW // HD:
                    val = rope(val, cos_s[g], sin_s[g])
                    k_s[g] = val.astype(BF16)
                    kt_s[tile, :, lanes] = val.T.astype(BF16)
                else:
                    v_s[g] = val.astype(BF16)
                    vt_s[tile, :, lanes] = val.T.astype(BF16)
        for g in pair:
            for n, (src, dst) in enumerate(out_copies(g)):
                pltpu.make_async_copy(src, dst, osem.at[n]).start()
            store_columns(full, nall, g, nall_sem)

        @pl.when(s == CHIPS)
        def _():
            @pl.loop(0, wt_s.shape[1] // HD)
            def _(j):
                wt_s[:, lanes_at(j, HD)] = w_s[lanes_at(j, HD), :].T

            pltpu.make_async_copy(wt_s, wt_out, wsem).start()
            rcopy(wt_s, wtp_out, wo_sem.at[TWO], wo_sem.at[TWO + ONE], p.partner).start()

    for n, (src, dst) in enumerate(whole):
        pltpu.make_async_copy(src, dst, osem.at[n]).wait()
    pltpu.make_async_copy(nall, nall, nall_sem).wait()
    pltpu.make_async_copy(wt_s, wt_out, wsem).wait()
    wo_copy.wait()
    rcopy(wt_s, wtp_out, wo_sem.at[TWO], wo_sem.at[TWO + ONE], p.partner).wait()
    for n, dev in enumerate(p.peers()):
        pos_copy(n, dev, dev).wait_send()
    ag_finish(p, *ag)


def attend_fwd_kernel(q, k, vt, posb, posr, wo, wop, x, gout, gain,
                      o_out, ot_out, lse_out, y_out, dproj_out, dgain_out, *scratch):
    n_rs = len(rs_scratch(BLK))
    rs, rest = scratch[:n_rs], scratch[n_rs:]
    (q_s, k_s, vt_s, posb_s, wo_s, gain_s, x_s, go_s, o_s, ot_s, op_s, part, qt, s_buf, e_buf, l_buf, acc, yst, dgain, row_a,
     row_b, lsem, op_ss, op_rs, osem, ysem) = rest
    fin, own = rs[HALF_PC], rs[HALF_PC + ONE]
    width = wo.shape[1]
    p = Place()
    loads = Loads(lsem)
    first = [loads.add(q, q_s), loads.add(k, k_s), loads.add(posb, posb_s), loads.add(vt, vt_s)]
    second = [loads.add(wo, wo_s.at[pl.ds(0, QW)]), loads.add(wop, wo_s.at[pl.ds(QW, QW)])]
    third = [loads.add(x, x_s), loads.add(gout, go_s), loads.add(gain, gain_s.at[0])]
    e_buf[...] = jnp.zeros_like(e_buf)
    barrier((p.right, p.left, p.partner))
    wait_all(first)

    def attend(pair, swap):
        walk = Walk(*pair)
        for n, g in enumerate(pair):
            qt[n] = q_s[:, g].reshape(TWO * BLK, HD).T
        acc[...] = jnp.zeros_like(acc)
        l_buf[...] = jnp.zeros_like(l_buf)

        def scores(i, a):
            n, _, t = walk.at(i)
            s_buf[a] = dot(k_s[t], qt[n])

        def values(i, a):
            n, _, t = walk.at(i)
            acc[n] += dot(vt_s[t], e_buf[a])

        def weights(i, a):
            n, g, t = walk.at(i)
            pos_q = walk.pos_q(i, posr[g])
            for c in range(KT // PIECE):
                keys = pl.ds(PIECE * c, PIECE)
                e = jnp.exp2(jnp.tanh(s_buf[a, keys, :] * (1.0 / SOFT_CAP)) * (SOFT_CAP * LOG2E))
                e = jnp.where(key_mask(pos_q, posb_s[t, keys, :]), e, 0.0)
                l_buf[n] += jnp.sum(e.reshape(PIECE // DEVS, DEVS, TWO * BLK), axis=0)
                e_buf[a, keys, :] = e.astype(BF16)

        def finish(n, g):
            l = jnp.sum(l_buf[n], axis=0, keepdims=True)
            lse_out[g] = jnp.log2(l)
            ot = acc[n] * (1.0 / l)
            for h in range(TWO):
                ot_s[h, :, lanes_at(g, BLK)] = ot[:, BLK * h:BLK * h + BLK].astype(BF16)
            o2 = ot.T.astype(BF16)
            for h in range(TWO):
                o_s[g, :, head(h)] = o2[BLK * h:BLK * h + BLK]

        scores(0, 0)

        @pl.loop(0, walk.turns)
        def _(turn):
            i = TWO * turn
            scores(i + ONE, ONE)
            values(i - ONE, ONE)
            weights(i, 0)
            scores(i + TWO, 0)
            values(i, 0)
            weights(i + ONE, ONE)

            @pl.when(lax.div(walk.na, TWO) == turn)
            def _():
                finish(0, walk.ga)
                swap.start()

        values(TWO * walk.turns - ONE, ONE)
        e_buf[...] = jnp.zeros_like(e_buf)
        finish(ONE, walk.gb)

    @pl.loop(0, RS_STEPS)
    def _(s):
        off, blk = pick(s, RS_OFF), pick(s, RS_BLK)
        chip = lax.rem(p.chip + off, CHIPS)
        mine = (TWO * chip + p.core) * NBLK + blk
        other = (TWO * chip + ONE - p.core) * NBLK + blk
        n = chip * NBLK + blk
        swap = rcopy(o_s.at[other], op_s.at[n], op_ss.at[n], op_rs.at[n], p.partner)
        attend((other, mine), swap)

        @pl.when(s == 0)
        def _():
            wait_all(second)

        swap.wait_recv()
        o_mine, o_part = o_s[mine], op_s[n]

        @pl.loop(0, TWO)
        def _(j):
            cols = lanes_at(j, width // TWO)
            part[:, cols] = dot(o_mine, wo_s[pl.ds(0, QW), cols]) + dot(o_part, wo_s[pl.ds(QW, QW), cols])

        rs_emit(p, s, part, *rs)

    outs = [pltpu.make_async_copy(o_s, o_out, osem.at[0]), pltpu.make_async_copy(ot_s, ot_out, osem.at[ONE])]
    for copy in outs:
        copy.start()
    wait_all(third)
    dgain[...] = jnp.zeros_like(dgain)
    for blk in RS_DONE:
        rs_wait_block(p, blk, *rs)

        @pl.loop(0, BLK // SUB)
        def _(r, blk=blk):
            rows, sums = rows16(r), []
            for cols in column_groups(width):
                val = rs_total(blk, r, cols, fin, own)
                row_a[:, cols] = val
                sums.append(fold(val * val))
            inv = lax.rsqrt(row_mean(sums, width) + NORM_EPS)
            sums = []
            for cols in column_groups(width):
                one_g = 1.0 + gain_s[:, cols]
                go = go_s[blk, rows, cols].astype(F32)
                nrm = row_a[:, cols] * inv
                post = (nrm * one_g).astype(BF16).astype(F32)
                yst[0, blk, rows, cols] = (x_s[blk, rows, cols].astype(F32) + post).astype(BF16)
                dg = go * nrm
                dgain[:, cols] += dg[:DEVS] + dg[DEVS:]
                gog = go * one_g
                row_a[:, cols] = nrm
                row_b[:, cols] = gog
                sums.append(fold(gog * nrm))
            mean = row_mean(sums, width)
            for cols in column_groups(width):
                yst[ONE, blk, rows, cols] = (inv * (row_b[:, cols] - row_a[:, cols] * mean)).astype(BF16)

        for n, dst in enumerate((y_out, dproj_out)):
            copy = pltpu.make_async_copy(yst.at[n, blk], dst.at[blk], ysem.at[n, blk])
            copy.start()
            outs.append(copy)
    dgain_out[...] = jnp.sum(dgain[...], axis=0, keepdims=True)
    for n in range(MY_BLK):
        rcopy(op_s.at[n], op_s.at[n], op_ss.at[n], op_rs.at[n], p.partner).wait_send()
    rs_finish(p, *rs)
    wait_all(outs)


def attend_bwd_kernel(q_scale, dproj, wo, q, k, kt, v, o, lse, cos_t, sin_t, posb, posr,
                      dall, dqkv_out, *scratch):
    n_ag = len(ag_scratch(BLK))
    ag, rest = scratch[:n_ag], scratch[n_ag:]
    (wo_s, q_s, k_s, kt_s, v_s, o_s, cos_s, sin_s, posb_s, dk_s, dv_s, dq_acc, out_s, qt, do_buf, dot_buf, delta, s_buf,
     dp_buf, p_buf, ds_buf, lsem, osem, own_sem) = rest
    full = ag[0]
    p = Place()
    loads = Loads(lsem)
    barrier((p.right, p.left, p.partner))

    def own_send(way, i):
        ag_send(p, way, i, dproj.at[i // TWO, half_of(i), :], *ag)

    for pieces in zip(*AG_FIRST):
        for way, i in enumerate(pieces):
            own_send(way, int(i))
    for b in range(NBLK):
        ag_swap(p, p.chip, b, dproj.at[b], full.at[p.me * NBLK + b], *ag).start()
    own = pltpu.make_async_copy(dproj, full.at[pl.ds(p.me * NBLK, NBLK)], own_sem)
    own.start()
    for src, dst in ((wo, wo_s), (o, o_s), (q, q_s), (k, k_s), (kt, kt_s), (v, v_s), (posb, posb_s), (cos_t, cos_s),
                     (sin_t, sin_s)):
        loads.add(src, dst)
    dk_s[...] = jnp.zeros_like(dk_s)
    dv_s[...] = jnp.zeros_like(dv_s)
    p_buf[...] = jnp.zeros_like(p_buf)
    ds_buf[...] = jnp.zeros_like(ds_buf)
    own.wait()
    for n, (src, dst) in enumerate(((wo, wo_s), (o, o_s), (q, q_s), (k, k_s), (kt, kt_s), (v, v_s), (posb, posb_s),
                                    (cos_t, cos_s), (sin_t, sin_s))):
        pltpu.make_async_copy(src, dst, lsem.at[n]).wait()
    dq_cols, kv_cols = pl.ds(0, QW), pl.ds(QW, QW)

    @pl.loop(0, AG_STEPS)
    def _(s):
        pair = [ag_step(p, s, n, *ag) for n in range(TWO)]
        ag_then(s, own_send)
        walk = Walk(*pair)
        for g in pair:
            store_columns(full, dall, g, osem.at[0])
        rows = jnp.concatenate([full[g] for g in pair], axis=0)
        do_all = dot_bt(rows, wo_s[...]).astype(BF16)
        for n, g in enumerate(pair):
            do2 = heads_down(do_all[BLK * n:BLK * n + BLK])
            do_buf[n] = do2
            dot_buf[n] = do2.T
            prod = do2.astype(F32) * heads_down(o_s[g]).astype(F32)
            delta[n] = jnp.sum(prod.T, axis=0, keepdims=True)
            qt[n] = q_s[:, g].reshape(TWO * BLK, HD).T
        dq_acc[...] = jnp.zeros_like(dq_acc)

        def scores(i, a):
            n, _, t = walk.at(i)
            s_buf[a] = dot(k_s[t], qt[n])
            dp_buf[a] = dot(v_s[t], dot_buf[n])

        def products(i, a):
            n, g, t = walk.at(i)
            dv_s[t] += dot(p_buf[a], do_buf[n])
            dk_s[t] += dot(ds_buf[a], q_s[:, g].reshape(TWO * BLK, HD))
            dq_acc[n] += dot(kt_s[t], ds_buf[a])

        def weights(i, a):
            n, g, t = walk.at(i)
            pos_q = walk.pos_q(i, posr[g])
            for c in range(KT // PIECE):
                keys = pl.ds(PIECE * c, PIECE)
                th = jnp.tanh(s_buf[a, keys, :] * (1.0 / SOFT_CAP))
                pr = jnp.exp2(th * (SOFT_CAP * LOG2E) - lse[g])
                pr = jnp.where(key_mask(pos_q, posb_s[t, keys, :]), pr, 0.0)
                p_buf[a, keys, :] = pr.astype(BF16)
                ds_buf[a, keys, :] = (pr * (dp_buf[a, keys, :] - delta[n]) * (1.0 - th * th)).astype(BF16)

        scores(0, 0)

        @pl.loop(0, walk.turns)
        def _(turn):
            i = TWO * turn
            scores(i + ONE, ONE)
            products(i - ONE, ONE)
            weights(i, 0)
            scores(i + TWO, 0)
            products(i, 0)
            weights(i + ONE, ONE)

        products(TWO * walk.turns - ONE, ONE)
        p_buf[...] = jnp.zeros_like(p_buf)
        ds_buf[...] = jnp.zeros_like(ds_buf)
        for n, g in enumerate(pair):
            dq = dq_acc[n].T
            for h in range(TWO):
                dq_h = rope_back(dq[BLK * h:BLK * h + BLK], cos_s[g], sin_s[g]) * q_scale
                out_s[g, :, head(h)] = dq_h.astype(BF16)
            pltpu.make_async_copy(out_s.at[g, :, dq_cols], dqkv_out.at[g, :, dq_cols], osem.at[ONE]).start()

    @pl.loop(0, ALL_BLK, unroll=CHIPS)
    def _(g):
        tile, rows = lax.div(g * BLK, KT), pl.ds(lax.rem(g, KT // BLK) * BLK, BLK)
        out_s[g, :, pl.ds(QW, HD)] = rope_back(dk_s[tile, rows, :], cos_s[g], sin_s[g]).astype(BF16)
        out_s[g, :, pl.ds(QW + HD, HD)] = dv_s[tile, rows, :].astype(BF16)
        pltpu.make_async_copy(out_s.at[g, :, kv_cols], dqkv_out.at[g, :, kv_cols], osem.at[TWO]).start()

    pltpu.make_async_copy(dall, dall, osem.at[0]).wait()
    pltpu.make_async_copy(out_s.at[:, :, dq_cols], dqkv_out.at[:, :, dq_cols], osem.at[ONE]).wait()
    pltpu.make_async_copy(out_s.at[:, :, kv_cols], dqkv_out.at[:, :, kv_cols], osem.at[TWO]).wait()
    ag_finish(p, *ag)


HOP_PLAN = ['O23', 'O01', 'O54', 'R54', 'L01', 'X01', 'X23', 'X45', 'R32', 'L23', 'R01', 'L54']
HOP_OFF, HOP_BLK = plan_tables(HOP_PLAN)
W_AHEAD = CHIPS
HOP_LATE = RS_STEPS - TWO
GROUPS = (digits('0145'), digits('23'))


def hop_emit(p, step, part, sent, turn, hop_l, hop_r, ss, hl_rs, hr_rs, result):
    kind = HOP_PLAN[step][0]
    for i in digits(HOP_PLAN[step][ONE:]):
        low, j = i < HALF_PC, i % HALF_PC
        hop, hop_rs, dev = (hop_l, hl_rs, p.right) if low else (hop_r, hr_rs, p.left)
        if kind == 'O':
            put_rows(part, sent.at[i], i)
            rcopy(sent.at[i], hop.at[j], ss.at[i], hop_rs.at[j], dev).start()
            continue
        n = 'RLX'.index(kind)
        if (kind == 'R' and low) or (kind == 'L' and not low):
            rcopy(hop.at[j], hop.at[j], ss.at[i], hop_rs.at[j], dev).wait_recv()
            put_rows(part, turn.at[n, i], i, hop.at[j])
        else:
            put_rows(part, turn.at[n, i], i)
        result(n, i).start()


def grad_rows_kernel(dqkv, wt, wtp, dg_post, *refs):
    n_out = TWO * len(GROUPS)
    hop_outs, (own_out, gpost_out), scratch = refs[:n_out], refs[n_out:n_out + TWO], refs[n_out + TWO:]
    (sent, turn, hop_l, hop_r, wt_s, d_s, dp_s, part, gains, ss, hl_rs, hr_rs, wt_sem, d_sem, dp_ss, dp_rs, out_sem, g_ss,
     g_rs, gsem) = scratch
    width = wt.shape[1]
    half, groups = width // TWO, width // QW
    p = Place()

    def w_loads(j):
        cols = lanes_at(j, QW)
        return [pltpu.make_async_copy(wt.at[:, cols], wt_s.at[pl.ds(0, QKV), cols], wt_sem.at[0, j]),
                pltpu.make_async_copy(wtp.at[:, cols], wt_s.at[pl.ds(QKV, QKV), cols], wt_sem.at[ONE, j])]

    def w_start(j):
        for copy in w_loads(j):
            copy.start()

    def block_of(off, blk, flip):
        chip = lax.rem(p.chip + off, CHIPS)
        return (TWO * chip + lax.rem(p.core + flip, TWO)) * NBLK + blk, chip * NBLK + blk

    def d_load(off, blk):
        g, n = block_of(off, blk, 0)
        return pltpu.make_async_copy(dqkv.at[g], d_s.at[n], d_sem.at[n])

    def d_swap(off, blk):
        other, n = block_of(off, blk, ONE)
        rcopy(dqkv.at[other], dp_s.at[n], dp_ss.at[n], dp_rs.at[n], p.partner).start()

    def result(n, i):
        dst = own_out.at[i]
        if n != TWO:
            group = [i in pieces for pieces in GROUPS].index(True)
            dst = hop_outs[n * len(GROUPS) + group].at[GROUPS[group].index(i)]
        return pltpu.make_async_copy(turn.at[n, i], dst, out_sem.at[n, i])

    plan = list(zip(HOP_OFF, HOP_BLK))
    d_load(*plan[0]).start()
    for j in range(W_AHEAD):
        w_start(j)
    barrier(p.peers())
    d_swap(*plan[0])
    send_gains(p, dg_post, gains, g_ss, g_rs)

    @pl.loop(0, RS_STEPS)
    def _(s):
        off, blk = pick(s, HOP_OFF), pick(s, HOP_BLK)
        _, n = block_of(off, blk, 0)
        late = jnp.where(s == HOP_LATE, I32(ONE), I32(0))
        d_load(off, blk).wait()
        rcopy(dp_s.at[n], dp_s.at[n], dp_ss.at[n], dp_rs.at[n], p.partner).wait_recv()
        d_mine, d_part = d_s[n], dp_s[n]

        def columns(cols):
            part[late, :, cols] = (dot(d_mine, wt_s[pl.ds(0, QKV), cols])
                                   + dot(d_part, wt_s[pl.ds(QKV, QKV), cols]))

        @pl.when(s == 0)
        def _():
            @pl.loop(0, groups)
            def _(j):
                @pl.when(j + W_AHEAD < groups)
                def _():
                    w_start(j + W_AHEAD)

                @pl.when(j + W_AHEAD == groups)
                def _():
                    for step in plan[ONE:]:
                        d_load(*step).start()
                        d_swap(*step)

                wait_all(w_loads(j))
                columns(lanes_at(j, QW))

        @pl.when(s != 0)
        def _():
            @pl.loop(0, TWO)
            def _(j):
                columns(lanes_at(j, half))

        @pl.when(s == RS_PLAN.index('X01'))
        def _():
            gain_total(p, dg_post, gains, gpost_out, g_ss, g_rs, gsem)

        for step in range(RS_STEPS):
            if step != HOP_LATE:
                @pl.when(s == step)
                def _(step=step):
                    if step > HOP_LATE:
                        hop_emit(p, HOP_LATE, part.at[ONE], sent, turn, hop_l, hop_r, ss, hl_rs, hr_rs, result)
                    hop_emit(p, step, part.at[0], sent, turn, hop_l, hop_r, ss, hl_rs, hr_rs, result)

    for i in range(NPC):
        rcopy(sent.at[i], sent.at[i], ss.at[i], hl_rs.at[0], p.right).wait_send()
    for n in range(MY_BLK):
        rcopy(dp_s.at[n], dp_s.at[n], dp_ss.at[n], dp_rs.at[n], p.partner).wait_send()
    for n in range(HALF_PC):
        for i in range(NPC):
            result(n, i).wait()


def gain_copy(n, src, gains, dev, owner, g_ss, g_rs):
    return rcopy(src, gains.at[owner], g_ss.at[n], g_rs.at[owner], dev)


def send_gains(p, src, gains, g_ss, g_rs):
    gains[p.me] = src[...]
    for n, dev in enumerate(p.peers()):
        gain_copy(n, src, gains, dev, p.me, g_ss, g_rs).start()


def gain_total(p, src, gains, out, g_ss, g_rs, gsem):
    for n, dev in enumerate(p.peers()):
        gain_copy(n, src, gains, dev, dev, g_ss, g_rs).wait()
    total = gains[0]
    for i in range(ONE, DEVS):
        total = total + gains[i]
    gains[p.me] = total
    copy = pltpu.make_async_copy(gains.at[p.me, 0], out, gsem)
    copy.start()
    copy.wait()


def weight_grads_kernel(dqkv, nall, dall, ot, y, gq_out, gk_out, gv_out, gwo_out, y_out, *scratch):
    d_s, in_s, gq_s, ot_s, gwo_s, y_s, lsem, isem, osem, wsem, ysem = scratch
    n_chunk = nall.shape[0]
    loads = Loads(lsem)
    first, second = loads.add(ot, ot_s), loads.add(y, y_s)
    d_copy = loads.add(dqkv, d_s)

    ahead = in_s.shape[0] - ONE

    def fetch(src, j, slot):
        pltpu.make_async_copy(src.at[j], in_s.at[slot], isem.at[slot]).start()

    def gwo_copies(j, slot):
        return [pltpu.make_async_copy(gwo_s.at[slot], gwo_out.at[:, lanes_at(j, HD)], wsem.at[slot])]

    def qkv_copies(j, slot):
        rows = lanes_at(j, HD)
        outs = (gq_out.at[rows, 0, :], gq_out.at[rows, ONE, :], gk_out.at[rows, 0, :], gv_out.at[rows, 0, :])
        return [pltpu.make_async_copy(gq_s.at[slot, :, head(n)], dst, osem.at[slot, n]) for n, dst in enumerate(outs)]

    def wo_chunk(a, slot):
        gwo_s[slot] = dot(ot_s[...], a)

    def qkv_chunk(a, slot):
        for h in range(TWO):
            cols = pl.ds(QW * h, QW)
            gq_s[slot, :, cols] = dot_at(a, d_s[:, :, cols].reshape(ALL_BLK * BLK, QW))

    def weight_grad(src, begun, after, compute, copies):
        @pl.loop(0, n_chunk)
        def _(j):
            at, slot = lax.rem(begun + j, ahead + ONE), lax.rem(j, TWO)
            pltpu.make_async_copy(src.at[j], in_s.at[at], isem.at[at]).wait()
            free = lax.rem(begun + j + ahead, ahead + ONE)

            @pl.when(j + ahead < n_chunk)
            def _():
                fetch(src, j + ahead, free)

            if after is not None:
                @pl.when(j + ahead >= n_chunk)
                def _():
                    fetch(after, j + ahead - n_chunk, free)

            @pl.when(j >= TWO)
            def _():
                wait_all(copies(j - TWO, slot))

            compute(in_s[at], slot)
            for copy in copies(j, slot):
                copy.start()

    for j in range(ahead):
        fetch(dall, j, j)
    first.wait()
    weight_grad(dall, 0, nall, wo_chunk, gwo_copies)
    d_copy.wait()
    second.wait()
    y_copy = pltpu.make_async_copy(y_s, y_out, ysem)
    y_copy.start()
    weight_grad(nall, n_chunk, None, qkv_chunk, qkv_copies)
    for j in (n_chunk - TWO, n_chunk - ONE):
        wait_all(gwo_copies(j, j % TWO) + qkv_copies(j, j % TWO))
    y_copy.wait()


def pre_load(pieces, from_left, from_right, own, x, gout, blocks, lsem):
    copies = []
    for m, i in enumerate(pieces):
        srcs = (from_left.at[m], from_right.at[m], own.at[i], x.at[i], gout.at[i])
        copies.append([pltpu.make_async_copy(src, blocks.at[n, m], lsem.at[n, m]) for n, src in enumerate(srcs)])
        for copy in copies[m]:
            copy.start()
    return copies


def pre_sums(blocks, m, gain, dn_s, stat, dgain):
    from_left, from_right, own, x, _ = (blocks.at[n, m] for n in range(blocks.shape[0]))
    width = x.shape[1]

    @pl.loop(0, PIECE // SUB)
    def _(r):
        rows, sums, dots = rows16(r), [], []
        for cols in column_groups(width):
            val = x[rows, cols].astype(F32)
            dn = (own[rows, cols].astype(F32) + from_left[rows, cols].astype(F32)
                  + from_right[rows, cols].astype(F32)).astype(BF16).astype(F32)
            dn_s[m, rows, cols] = dn
            sums.append(fold(val * val))
            dots.append(fold(dn * (1.0 + gain[:, cols]) * val))
        inv = lax.rsqrt(row_mean(sums, width) + NORM_EPS)
        stat[0, m, rows, :] = jnp.broadcast_to(inv, (SUB, HD2))
        stat[ONE, m, rows, :] = jnp.broadcast_to(row_mean(dots, width) * inv, (SUB, HD2))
        for cols in column_groups(width):
            dg = dn_s[m, rows, cols] * (x[rows, cols].astype(F32) * inv)
            dgain[:, cols] += dg[:DEVS] + dg[DEVS:]


def pre_result(blocks, m, gain, dn_s, stat, gx):
    x, gout = blocks.at[NBLK, m], blocks.at[NBLK + ONE, m]

    @pl.loop(0, PIECE // SUB)
    def _(r):
        rows = rows16(r)
        inv, mean = stat[0, m, rows, 0:1], stat[ONE, m, rows, 0:1]
        for cols in column_groups(x.shape[1]):
            nrm = x[rows, cols].astype(F32) * inv
            dx = (inv * (dn_s[m, rows, cols] * (1.0 + gain[:, cols]) - nrm * mean)).astype(BF16).astype(F32)
            gx[m, rows, cols] = (gout[rows, cols].astype(F32) + dx).astype(BF16)


def pre_grad_kernel(pieces, from_left, from_right, own, x, gout, gain, gx_out, dgain, blocks, gain_s, dn_s, stat, gx, lsem,
                    xsem, gsem):
    copies = pre_load(pieces, from_left, from_right, own, x, gout, blocks, lsem)
    gain_in = pltpu.make_async_copy(gain, gain_s.at[0], gsem)
    gain_in.start()
    dgain[...] = jnp.zeros_like(dgain)
    gain_in.wait()
    for m, i in enumerate(pieces):
        wait_all(copies[m])
        pre_sums(blocks, m, gain_s, dn_s, stat, dgain)
        pre_result(blocks, m, gain_s, dn_s, stat, gx)
        pltpu.make_async_copy(gx.at[m], gx_out.at[i], xsem.at[m]).start()
    for m, i in enumerate(pieces):
        pltpu.make_async_copy(gx.at[m], gx_out.at[i], xsem.at[m]).wait()


def pre_scratch(n, width):
    return [pltpu.VMEM((NBLK + TWO, n, PIECE, width), BF16), pltpu.VMEM((ONE, width), F32),
            pltpu.VMEM((n, PIECE, width), F32), pltpu.VMEM((TWO, n, PIECE, HD2), F32), pltpu.VMEM((n, PIECE, width), BF16),
            pltpu.SemaphoreType.DMA((NBLK + TWO, n))]


def pre_grad(pieces, *args):
    x, dma = args[NBLK], pltpu.SemaphoreType.DMA
    width = x.shape[TWO]
    return pl.pallas_call(
        functools.partial(pre_grad_kernel, pieces), name='pre_grad',
        out_shape=(sds(x.shape, BF16), sds((DEVS, width), F32)), in_specs=specs('AAAAAA'), out_specs=specs('AV'),
        scratch_shapes=pre_scratch(len(pieces), width) + [dma((len(pieces),)), dma(())],
        compiler_params=pltpu.CompilerParams(vmem_limit_bytes=VMEM_BYTES))(*args)


def last_rows_kernel(from_left, from_right, own, x, gout, gain, dgain_in, gx_out, gpre_out, *scratch):
    blocks, gain_s, dn_s, stat, gx, psem, dgain, row, gains, lsem, xsem, g_ss, g_rs, gsem = scratch
    pieces = GROUPS[ONE]
    p = Place()
    copies = pre_load(pieces, from_left, from_right, own, x, gout, blocks, psem)
    loads = Loads(lsem)
    rest = [loads.add(gain, gain_s.at[0]), loads.add(dgain_in, dgain)]
    barrier(p.peers())
    wait_all(rest)
    for m in range(len(pieces)):
        wait_all(copies[m])
        pre_sums(blocks, m, gain_s, dn_s, stat, dgain)
    row[...] = jnp.sum(dgain[...], axis=0, keepdims=True)
    send_gains(p, row, gains, g_ss, g_rs)
    for m in range(len(pieces)):
        pre_result(blocks, m, gain_s, dn_s, stat, gx)
    result = pltpu.make_async_copy(gx, gx_out, xsem)
    result.start()
    gain_total(p, row, gains, gpre_out, g_ss, g_rs, gsem)
    result.wait()


def finish_kernel(gx_last, gpre, gpost, gx_in, gx_out, gpre_out, gpost_out, blk_s, pre_s, post_s, get, put):
    moves = ((gx_last, blk_s, gx_out.at[pl.ds(GROUPS[ONE][0], len(GROUPS[ONE]))]), (gpre, pre_s, gpre_out), (gpost, post_s, gpost_out))
    for n, (src, buf, dst) in enumerate(moves):
        pltpu.make_async_copy(src, buf, get.at[n]).start()
    for n, (src, buf, dst) in enumerate(moves):
        pltpu.make_async_copy(src, buf, get.at[n]).wait()
        pltpu.make_async_copy(buf, dst, put.at[n]).start()
    for n, (src, buf, dst) in enumerate(moves):
        pltpu.make_async_copy(buf, dst, put.at[n]).wait()


def specs(places):
    return [pl.BlockSpec(memory_space={'A': pl.ANY, 'V': pltpu.VMEM}[place]) for place in places]


def params(cid):
    return pltpu.CompilerParams(collective_id=cid, has_side_effects=True, vmem_limit_bytes=VMEM_BYTES)


def sds(shape, dtype):
    return jax.ShapeDtypeStruct(shape, dtype)


def solution(mesh):
    act_spec = P('dp', 'tp', None)
    head_spec = P(None, 'tp', None)
    grad_spec = P('dp', 'tp', None)
    in_specs = (act_spec, P('dp', 'tp'), act_spec, head_spec, head_spec, head_spec, P('tp', None, None), P(None), P(None))
    out_specs = (act_spec, act_spec, grad_spec, grad_spec, grad_spec, P(('dp', 'tp'), None, None), P('dp'), P('dp'))
    assert mesh.shape['tp'] == DEVS

    def local_step(x_in, positions, grad_out, w_query, w_key, w_value, w_out, gain_pre, gain_post):
        width, _, head_dim = w_query.shape
        q_scale = head_dim ** -0.5
        rows = ALL_BLK * BLK
        tiles = rows // KT
        dma = pltpu.SemaphoreType.DMA
        vm = pltpu.VMEM
        x_blk = x_in.reshape(NBLK, BLK, width)
        go_blk = grad_out.reshape(NBLK, BLK, width)
        wo = w_out.reshape(QW, width)
        inv_freq = (ROPE_THETA ** (-2.0 * np.arange(HD2) / head_dim)).astype(np.float32).reshape(ONE, HD2)

        all_bf, rope_t = sds((width // HD, ALL_BLK, BLK, HD), BF16), sds((ALL_BLK, BLK, HD2), F32)
        blocks, tiles_t = sds((ALL_BLK, BLK, HD), BF16), sds((tiles, HD, KT), BF16)
        pos_blk, pos_row = sds((ALL_BLK, BLK, HD2), I32), sds((ALL_BLK, ONE, HD2), I32)
        q_all, w_t, own_rows = sds((TWO, ALL_BLK, BLK, HD), BF16), sds((QKV, width), BF16), sds(x_blk.shape, BF16)
        o_all, ot_all, lse_all = sds((ALL_BLK, BLK, QW), BF16), sds((TWO, HD, rows), BF16), sds((ALL_BLK, ONE, HD), F32)
        d_all, gain_row = sds((ALL_BLK, BLK, QKV), BF16), sds((ONE, width), F32)

        def like(*specs):
            return [vm(spec.shape, spec.dtype) for spec in specs]

        (nall, q, k, v, kt, vt, cos_t, sin_t, posb, posr, wt, wtp, wop) = pl.pallas_call(
            functools.partial(gather_qkv_kernel, q_scale), name='gather_qkv',
            out_shape=(all_bf, q_all, blocks, blocks, tiles_t, tiles_t, rope_t, rope_t, pos_blk, pos_row, w_t, w_t,
                       sds(wo.shape, BF16)),
            in_specs=specs('AVVAAAAA'), out_specs=specs('AAAAAAAAAVAAA'),
            scratch_shapes=ag_scratch(width) + like(
                own_rows, gain_row, sds(w_query.shape, BF16), sds((width, QKV), BF16), w_t, q_all, blocks, blocks, tiles_t, tiles_t, rope_t, rope_t,
                pos_blk, pos_row) + [dma((10,)), dma((9,)), dma(()), dma((CHIPS,)), dma((DEVS,)), dma((DEVS,)), dma(())],
            compiler_params=params(0),
        )(x_blk, positions.reshape(NBLK, ONE, BLK), inv_freq, gain_pre, w_query, w_key.reshape(width, HD), w_value.reshape(width, HD), wo)

        k_t, v_t, posb_t = (a.reshape(tiles, KT, a.shape[2]) for a in (k, v, posb))
        tile_rows, tile_f = sds(k_t.shape, BF16), sds(k_t.shape, F32)
        tile_pos, score, square = sds(posb_t.shape, I32), sds((TWO, KT, HD), F32), sds((TWO, HD, HD), BF16)
        square_f, part = sds((TWO, HD, HD), F32), sds((BLK, width), F32)
        o, ot, lse, y, dproj, dg_post = pl.pallas_call(
            attend_fwd_kernel, name='attend_fwd',
            out_shape=(o_all, ot_all, lse_all, own_rows, own_rows, gain_row),
            in_specs=specs('AAAAVAAAAA'), out_specs=specs('AAVAAV'),
            scratch_shapes=rs_scratch(width) + like(
                q_all, tile_rows, tiles_t, tile_pos, w_t, gain_row, own_rows, own_rows, o_all, ot_all,
                sds((MY_BLK, BLK, QW), BF16), part, square, score, sds(score.shape, BF16), sds((TWO, DEVS, HD), F32),
                square_f, sds((TWO,) + x_blk.shape, BF16), sds((DEVS, width), F32), sds((SUB, width), F32),
                sds((SUB, width), F32))
            + [dma((9,)), dma((MY_BLK,)), dma((MY_BLK,)), dma((TWO,)), dma((TWO, NBLK))],
            compiler_params=params(1),
        )(q, k_t, vt, posb_t, posr, wo, wop, x_blk, go_blk, gain_post)

        dall, dqkv = pl.pallas_call(
            functools.partial(attend_bwd_kernel, q_scale), name='attend_bwd',
            out_shape=(all_bf, d_all),
            in_specs=specs('AAAAAAAVAAAV'), out_specs=specs('AA'),
            scratch_shapes=ag_scratch(width) + like(
                sds(wo.shape, BF16), q_all, tile_rows, tiles_t, tile_rows, o_all, rope_t, rope_t, tile_pos, tile_f, tile_f,
                square_f, d_all, square, square, square, sds((TWO, ONE, HD), F32), score, score, sds(score.shape, BF16),
                sds(score.shape, BF16)) + [dma((9,)), dma((3,)), dma(())],
            compiler_params=params(2),
        )(dproj, wo, q, k_t, kt, v_t, o, lse, cos_t, sin_t, posb_t, posr)

        hops = [sds((len(pieces), PIECE, width), BF16) for pieces in GROUPS]
        piece, own_pieces = sds((HALF_PC, PIECE, width), BF16), sds((NPC, PIECE, width), BF16)
        gain_all, d_mine = sds((DEVS, ONE, width), F32), sds((MY_BLK, BLK, QKV), BF16)
        *to_all, own, gpost = pl.pallas_call(
            grad_rows_kernel, name='grad_rows',
            out_shape=hops + hops + [own_pieces, sds((width,), F32)],
            in_specs=specs('AAAV'), out_specs=specs('AAAAAA'),
            scratch_shapes=like(
                own_pieces, sds((HALF_PC, NPC, PIECE, width), BF16), piece, piece,
                sds((TWO * QKV, width), BF16), d_mine, d_mine, sds((TWO, BLK, width), F32), gain_all)
            + [dma((NPC,)), dma((HALF_PC,)), dma((HALF_PC,)), dma((TWO, width // QW)), dma((MY_BLK,)),
               dma((MY_BLK,)), dma((MY_BLK,)), dma((HALF_PC, NPC)), dma((DEVS,)), dma((DEVS,)), dma(())],
            compiler_params=params(3),
        )(dqkv, wt, wtp, dg_post)

        def shift(rows_out, way):
            ring = [(TWO * c + k, TWO * ((c + way) % CHIPS) + k) for c in range(CHIPS) for k in range(TWO)]
            return lax.ppermute(rows_out, 'tp', ring)

        hops_in = []
        for n in range(len(GROUPS)):
            hops_in.append((shift(to_all[n], ONE), shift(to_all[n + len(GROUPS)], CHIPS - ONE)))
        flops = TWO * rows * width * (QKV + QW)
        gq, gk, gv, gwo, y = pl.pallas_call(
            weight_grads_kernel, name='weight_grads',
            out_shape=(sds(w_query.shape, F32), sds(w_key.shape, F32), sds(w_value.shape, F32), sds(wo.shape, F32),
                       own_rows),
            in_specs=specs('AAAAA'), out_specs=specs('AAAAA'),
            scratch_shapes=like(
                d_all, sds((CHIPS, rows, HD), BF16), sds((TWO, HD, QKV), F32), sds((QW, rows), BF16), sds((TWO, QW, HD), F32),
                own_rows) + [dma((3,)), dma((CHIPS,)), dma((TWO, CHIPS)), dma((TWO,)), dma(())],
            cost_estimate=pl.CostEstimate(flops=flops, bytes_accessed=TWO * rows * width * CHIPS, transcendentals=0),
            compiler_params=pltpu.CompilerParams(vmem_limit_bytes=VMEM_BYTES),
        )(dqkv, *(a.reshape(width // HD, rows, HD) for a in (nall, dall)), ot.reshape(QW, rows), y)
        x_pc, go_pc = x_in.reshape(NPC, PIECE, width), grad_out.reshape(NPC, PIECE, width)
        gx, dgain = pre_grad(GROUPS[0], *hops_in[0], own, x_pc, go_pc, gain_pre)
        block = hops[ONE]
        gx_last, gpre = pl.pallas_call(
            last_rows_kernel, name='last_rows', out_shape=(block, sds((width,), F32)),
            in_specs=specs('AAAAAAA'), out_specs=specs('AA'),
            scratch_shapes=pre_scratch(block.shape[0], width) + like(sds((DEVS, width), F32), gain_row, gain_all)
            + [dma((TWO,)), dma(()), dma((DEVS,)), dma((DEVS,)), dma(())],
            compiler_params=params(4),
        )(*hops_in[ONE], own, x_pc, go_pc, gain_pre, dgain)
        gx, gpre, gpost = pl.pallas_call(
            finish_kernel, name='finish', out_shape=(own_pieces, sds((width,), F32), sds((width,), F32)),
            in_specs=specs('AAAA'), out_specs=specs('AAA'), input_output_aliases={3: 0},
            scratch_shapes=like(block, sds((width,), F32), sds((width,), F32)) + [dma((3,)), dma((3,))],
            compiler_params=pltpu.CompilerParams(vmem_limit_bytes=VMEM_BYTES),
        )(gx_last, gpre, gpost, gx)
        return (y.reshape(x_in.shape), gx.reshape(x_in.shape), gq, gk, gv, gwo.reshape(w_out.shape), gpre, gpost)

    return jax.shard_map(local_step, mesh=mesh, in_specs=in_specs, out_specs=out_specs, check_vma=False)
```

time: 1420 us -> 448 us (0.32)
  matrix products: 767 us -> 0 us
  Pallas kernels: 0 us -> 428 us
  waiting for transfers between devices: 313 us -> 11.5 us
  other arithmetic: 160 us -> 0 us
  local copies, waits for them, and re-layouts: 123 us -> 0 us
  blocking collectives: 38 us -> 0 us
    dot_general x180 -> x0, matrix products: 767 us -> none  [the longest x48 126 us: block_probs(): jnp.einsum('bqkgd,bskd->bkgqs', q_blk, k_blk, preferred_element_type=jnp....]
    pallas_call x0 -> x8, Pallas kernels: none -> 428 us  [the longest x1 109 us: local_step(): pl.pallas_call(functools.partial(attend_bwd_kernel, q_scale), name='atten...]
    all_gather x2 -> x0, waiting for transfers between devices: 191 us -> none  [the longest x1 104 us: local_step(): d_proj_all = lax.all_gather(d_proj, 'tp', axis=1, tiled=True)]
    reduce_scatter x2 -> x0, waiting for transfers between devices: 122 us -> none  [the longest x1 114 us: local_step(): lax.psum_scatter(part_proj.astype(jnp.bfloat16), 'tp', scatter_dimension=...]
    dynamic_update_slice x48 -> x0, local copies, waits for them, and re-layouts: 60.3 us -> none  [block_step(): d_q = lax.dynamic_update_slice_in_dim(d_q, dq_blk, q_start, axis=1)]
    reduce_sum x52 -> x0, other arithmetic: 51.6 us -> none  [the longest x48 34.7 us: block_probs(): jax.nn.softmax(jnp.where(in_window, capped, -1e+30), axis=-1)]
    unnamed x49 -> x0, local copies, waits for them, and re-layouts: 49.5 us -> none
    another operation x25 -> x0, other arithmetic: 44.6 us -> none
  transfers between devices with their start and end apart: 4 -> 4, of which waited for: 4 -> 1; matrix products, arithmetic and copies ran while one was open for 8% -> 0% of each run, Pallas kernels for 0% -> 12%
where the time goes in v1:
time: 448 us; the launch traced here: 447 us
  Pallas kernels  428 us (96%)
  waiting for transfers between devices  11.5 us (3%)
  starting transfers between devices  6.56 us (1%)
    pallas_call x1, Pallas kernels, local_step(): pl.pallas_call(functools.partial(attend_bwd_kernel, q_scale), name='atten...  109 us
    pallas_call x1, Pallas kernels, local_step(): pl.pallas_call(attend_fwd_kernel, name='attend_fwd', out_shape=(o_all, ot...  107 us
    pallas_call x1, Pallas kernels, local_step(): pl.pallas_call(functools.partial(gather_qkv_kernel, q_scale), name='gathe...  102 us
    pallas_call x1, Pallas kernels, local_step(): pl.pallas_call(weight_grads_kernel, name='weight_grads', out_shape=(sds(w...  44.9 us
    pallas_call x1, Pallas kernels, local_step(): pl.pallas_call(grad_rows_kernel, name='grad_rows', out_shape=hops + hops...  43.5 us
    ppermute x4, waiting for transfers between devices, shift(): return lax.ppermute(rows_out, 'tp', ring)  11.5 us
    pallas_call x1, Pallas kernels, pre_grad(): pl.pallas_call(functools.partial(pre_grad_kernel, pieces), name='pre_grad...  10.1 us
    pallas_call x1, Pallas kernels, local_step(): pl.pallas_call(last_rows_kernel, name='last_rows', out_shape=(block, sds(...  9.41 us
  transfers between devices with their start and end apart: 4, of which 1 were waited for; matrix products, arithmetic and copies ran while one was open for 0% of the time, Pallas kernels for 12%

profile of v1, /device:TPU:88, one launch (start us, length us, event | category | flops | bytes accessed | tf_op | source)
XLA Modules:
  0.0 447.0 jit_solution(8949431474789791020)
XLA Ops:
  0.6 102.2 %gather_qkv.1 = (bf16[14,24,128,256]{3,2,1,0:T(8,128)(2,1)}, bf16[2,24,128,256]{3,2,1,0:T(8,128)(2,1)}, bf16[24,128,256]{2,1,0:T(8,128)(2,1)}, bf16[24,128,256]{...) custom-call(bf16[3,128,3584]{2,1,0:T(8,128)(2,1)} %bitcast.17, ...), custom_call_target="tpu_custom_call" | custom-call | tf_op jit(solution)/shard_map/gather_qkv/pallas_call | solution.py:1091
  102.8 107.2 %attend_fwd.1 = (bf16[24,128,512]{2,1,0:T(8,128)(2,1)}, bf16[2,256,3072]{2,1,0:T(8,128)(2,1)}, f32[24,1,256]{2,1,0:T(1,128)}, bf16[3,128,3584]{2,1,0:T(8,128)(2,...) custom-call(bf16[2,24,128,256]{3,2,1,0:T(8,128)(2,1)} %get-tuple-element.47.q, bf16[6,512,256]{2,1,0:T(8,128)(2,1)} %bitcast.27, ...), custom_call_target="tpu_custom_call" | custom-call | tf_op jit(solution)/shard_map/attend_fwd/pallas_call | solution.py:1106
  210.0 108.6 %attend_bwd.1 = (bf16[14,24,128,256]{3,2,1,0:T(8,128)(2,1)}, bf16[24,128,1024]{2,1,0:T(8,128)(2,1)}) custom-call(bf16[3,128,3584]{2,1,0:T(8,128)(2,1)} %get-tuple-element.53.dproj, bf16[512,3584]{1,0:T(8,128)(2,1)} %bitcast.23, bf16[2,24,128,256]{3,2,1,0:T(8,128)(2,1)} %get-tuple-element.47.q, bf16[6,512,256]{2,1,0:T(8,128)(2,1)} %bitcast.28, ...), custom_call_target="tpu_custom_call" | custom-call | tf_op jit(solution)/shard_map/attend_bwd/pallas_call | solution.py:1119
  318.6 43.5 %grad_rows.1 = (bf16[4,64,3584]{2,1,0:T(8,128)(2,1)}, bf16[2,64,3584]{2,1,0:T(8,128)(2,1)}, bf16[4,64,3584]{2,1,0:T(8,128)(2,1)}, bf16[2,64,3584]{2,1,0:T(8,128)...) custom-call(bf16[24,128,1024]{2,1,0:T(8,128)(2,1)} %get-tuple-element.60.dqkv, ...), custom_call_target="tpu_custom_call" | custom-call | tf_op jit(solution)/shard_map/grad_rows/pallas_call | solution.py:1133
  362.1 0.1 collective-permute-start
  362.2 3.2 collective-permute-start.1
  365.4 0.0 collective-permute-start.2
  365.4 3.2 collective-permute-start.3
  368.7 44.9 %weight_grads.1 = (f32[3584,2,256]{2,1,0:T(2,128)}, f32[3584,1,256]{2,1,0:T(1,128)}, f32[3584,1,256]{2,1,0:T(1,128)}, f32[512,3584]{1,0:T(8,128)}, bf16[3,128,3584]{2,1,0:T(8,128)(2,1)}) custom-call(bf16[24,128,1024]{2,1,0:T(8,128)(2,1)} %get-tuple-element.60.dqkv, bf16[14,3072,256]{2,1,0:T(8,128)(2,1)} %bitcast.36, bf16[14,3072,256]{2,1,0:T(8,128)(2,1)} %bitcast.37, ...), custom_call_target="tpu_custom_call" | custom-call | flops 33822867456 | bytes 88080384 | tf_op jit(solution)/shard_map/weight_grads/pallas_call | solution.py:1153
  413.6 11.5 %collective-permute-done.2.from_left = bf16[4,64,3584]{2,1,0:T(8,128)(2,1)} collective-permute-done((bf16[4,64,3584]{2,1,0:T(8,128)(2,1)}, bf16[4,64,3584]{2,1,0:T(8,128)(2,1)}, u32[]{:S(2)}, u32[]{:S(2)}) %collective-permute-start.2) | collective-permute-done | bytes 1835040 | tf_op jit(solution)/shard_map/ppermute | solution.py:1147
  425.1 0.0 collective-permute-done.3.from_right
  425.1 10.1 %pre_grad.1 = (bf16[6,64,3584]{2,1,0:T(8,128)(2,1)}, f32[8,3584]{1,0:T(8,128)}) custom-call(bf16[4,64,3584]{2,1,0:T(8,128)(2,1)} %collective-permute-done.2.from_left, bf16[4,64,3584]{2,1,0:T(8,128)(2,1)} %collective-permute-done.3.from_right, bf16[6,64,3584]{2,1,0:T(8,128)(2,1)} %get-tuple-element.71.own, bf16[6,64,3584]{2,1,0:T(8,128)(2,1)} %bitcast.19, ...), custom_call_target="tpu_custom_call" | custom-call | tf_op jit(solution)/shard_map/pre_grad/pallas_call | solution.py:1009
  435.2 0.0 collective-permute-done.from_left
  435.2 0.0 collective-permute-done.1.from_right
  435.2 9.4 %last_rows.1 = (bf16[2,64,3584]{2,1,0:T(8,128)(2,1)}, f32[3584]{0:T(1024)}) custom-call(bf16[2,64,3584]{2,1,0:T(8,128)(2,1)} %collective-permute-done.from_left, bf16[2,64,3584]{2,1,0:T(8,128)(2,1)} %collective-permute-done.1.from_right, bf16[6,64,3584]{2,1,0:T(8,128)(2,1)} %get-tuple-element.71.own, bf16[6,64,3584]{2,1,0:T(8,128)(2,1)} %bitcast.20, ...), custom_call_target="tpu_custom_call" | custom-call | tf_op jit(solution)/shard_map/last_rows/pallas_call | solution.py:1167
  444.7 2.2 finish.1
Async XLA Ops:
  362.1 73.1 %collective-permute-start = (bf16[2,64,3584]{2,1,0:T(8,128)(2,1)}, bf16[2,64,3584]{2,1,0:T(8,128)(2,1)}, u32[]{:S(2)}, u32[]{:S(2)}) collective-permute-start(bf16[2,64,3584]{2,1,0:T(8,128)(2,1)} %get-tuple-element.69), channel_id=1, source_target_pairs={{0,2},{1,3},{2,4},{3,5},{4,6},{5,7},{6,0},{7,1},{8,10},{9,11},{10,... | collective-permute-start | bytes 2752520 | tf_op jit(solution)/shard_map/ppermute | solution.py:1147
  362.2 73.0 %collective-permute-start.1 = (bf16[2,64,3584]{2,1,0:T(8,128)(2,1)}, bf16[2,64,3584]{2,1,0:T(8,128)(2,1)}, u32[]{:S(2)}, u32[]{:S(2)}) collective-permute-start(bf16[2,64,3584]{2,1,0:T(8,128)(2,1)} %get-tuple-element.70), channel_id=1, source_target_pairs={{0,6},{1,7},{2,0},{3,1},{4,2},{5,3},{6,4},{7,5},{8,14},{9,15},{10,... | collective-permute-start | bytes 2752520 | tf_op jit(solution)/shard_map/ppermute | solution.py:1147
  365.4 59.7 %collective-permute-start.2 = (bf16[4,64,3584]{2,1,0:T(8,128)(2,1)}, bf16[4,64,3584]{2,1,0:T(8,128)(2,1)}, u32[]{:S(2)}, u32[]{:S(2)}) collective-permute-start(bf16[4,64,3584]{2,1,0:T(8,128)(2,1)} %get-tuple-element.72), channel_id=1, source_target_pairs={{0,2},{1,3},{2,4},{3,5},{4,6},{5,7},{6,0},{7,1},{8,10},{9,11},{10,... | collective-permute-start | bytes 5505032 | tf_op jit(solution)/shard_map/ppermute | solution.py:1147
  365.4 59.7 %collective-permute-start.3 = (bf16[4,64,3584]{2,1,0:T(8,128)(2,1)}, bf16[4,64,3584]{2,1,0:T(8,128)(2,1)}, u32[]{:S(2)}, u32[]{:S(2)}) collective-permute-start(bf16[4,64,3584]{2,1,0:T(8,128)(2,1)} %get-tuple-element.73), channel_id=1, source_target_pairs={{0,6},{1,7},{2,0},{3,1},{4,2},{5,3},{6,4},{7,5},{8,14},{9,15},{10,... | collective-permute-start | bytes 5505032 | tf_op jit(solution)/shard_map/ppermute | solution.py:1147

commit v2 on v1

--- a/solution.py
+++ b/solution.py
@@ -98,6 +98,7 @@
 AG_FLIP = (digits('000110101010'), digits('010110101011'))
 AG_BLK = (digits('020101100221'), digits('102221122001'))
 AG_STEPS = len(AG_OFF[0])
+AG_LAST = AG_STEPS - ONE
 AG_FORWARD = {2: ('01', '54'), 5: ('2', '3')}
 AG_FIRST = ('0123', '5432')
 AG_THEN = ('45', '10')
@@ -146,6 +147,18 @@
     return off, flip, chip, shard, blk, shard * NBLK + blk
 
 
+def ag_arrive(p, chip, blk, g, full, ring_rs, part_rs, own_ss, fwd_ss, part_ss):
+    for h in range(TWO):
+        half = full.at[g, half_of(h), :]
+        rcopy(half, half, fwd_ss.at[0], ring_rs.at[chip, TWO * blk + h], p.partner).wait_recv()
+    rcopy(full.at[g], full.at[g], part_ss.at[chip, blk], part_rs.at[chip, blk], p.partner).start()
+
+
+def ag_last(p, *ag):
+    _, _, chip, _, blk, g = ag_block(p, AG_LAST, 0)
+    ag_arrive(p, chip, blk, g, *ag)
+
+
 def ag_step(p, s, n, full, ring_rs, part_rs, own_ss, fwd_ss, part_ss):
     off, flip, chip, shard, blk, g = ag_block(p, s, n)
     swap = rcopy(full.at[g], full.at[g], part_ss.at[chip, blk], part_rs.at[chip, blk], p.partner)
@@ -154,12 +167,11 @@
     def _():
         swap.wait_recv()
 
-    @pl.when(jnp.logical_and(flip == 0, off != 0))
+    ring = jnp.logical_and(flip == 0, off != 0)
+
+    @pl.when(ring if n else jnp.logical_and(ring, s != AG_LAST))
     def _():
-        for h in range(TWO):
-            half = full.at[g, half_of(h), :]
-            rcopy(half, half, fwd_ss.at[0], ring_rs.at[chip, TWO * blk + h], p.partner).wait_recv()
-        swap.start()
+        ag_arrive(p, chip, blk, g, full, ring_rs, part_rs, own_ss, fwd_ss, part_ss)
 
     for step, pieces in AG_FORWARD.items():
         @pl.when(s == step)
@@ -248,7 +260,7 @@
             rcopy(fin.at[side, i], fin.at[side, i], ss.at[0, i], fin_rs.at[side, i], p.right).wait_recv()
 
 
-def rs_total(blk, r, cols, fin, own):
+def rs_total(blk, fin, own, r, cols):
     per = PIECE // SUB
     i, rows = TWO * blk + lax.div(r, per), rows16(lax.rem(r, per))
     total = (own[blk, rows16(r), cols].astype(F32) + fin[0, i, rows, cols].astype(F32)
@@ -272,6 +284,35 @@
     for part in parts[ONE:]:
         total = total + part
     return jnp.sum(total, axis=1, keepdims=True) * (1.0 / width)
+
+
+def post_rows(total, x, gout, gain, y, dproj, dgain, row_a, row_b):
+    width = x.shape[1]
+
+    @pl.loop(0, BLK // SUB)
+    def _(r):
+        rows, sums = rows16(r), []
+        for cols in column_groups(width):
+            val = total(r, cols)
+            row_a[:, cols] = val
+            sums.append(fold(val * val))
+        inv = lax.rsqrt(row_mean(sums, width) + NORM_EPS)
+        sums = []
+        for cols in column_groups(width):
+            one_g = 1.0 + gain[:, cols]
+            go = gout[rows, cols].astype(F32)
+            nrm = row_a[:, cols] * inv
+            post = (nrm * one_g).astype(BF16).astype(F32)
+            y[rows, cols] = (x[rows, cols].astype(F32) + post).astype(BF16)
+            dg = go * nrm
+            dgain[:, cols] += dg[:DEVS] + dg[DEVS:]
+            gog = go * one_g
+            row_a[:, cols] = nrm
+            row_b[:, cols] = gog
+            sums.append(fold(gog * nrm))
+        mean = row_mean(sums, width)
+        for cols in column_groups(width):
+            dproj[rows, cols] = (inv * (row_b[:, cols] - row_a[:, cols] * mean)).astype(BF16)
 
 
 def rs_finish(p, sent, hop_l, hop_r, fin, own, ss, hl_rs, hr_rs, fin_rs):
@@ -410,13 +451,39 @@
 
     def out_copies(g):
         tile, lanes = lax.div(g * BLK, KT), lanes_at(lax.rem(g, KT // BLK), BLK)
-        return [(q_s.at[:, g], q_out.at[:, g]), (k_s.at[g], k_out.at[g]),
-                (v_s.at[g], v_out.at[g]), (cos_s.at[g], cos_out.at[g]), (sin_s.at[g], sin_out.at[g]),
-                (posb_s.at[g], posb_out.at[g]), (kt_s.at[tile, :, lanes], kt_out.at[tile, :, lanes]),
-                (vt_s.at[tile, :, lanes], vt_out.at[tile, :, lanes])]
-
-    whole = [(q_s, q_out), (k_s, k_out), (v_s, v_out), (cos_s, cos_out), (sin_s, sin_out),
-             (posb_s, posb_out), (kt_s, kt_out), (vt_s, vt_out)]
+        return [(cos_s.at[g], cos_out.at[g]), (sin_s.at[g], sin_out.at[g]), (posb_s.at[g], posb_out.at[g]),
+                (q_s.at[:, g], q_out.at[:, g]), (k_s.at[g], k_out.at[g]), (v_s.at[g], v_out.at[g]),
+                (kt_s.at[tile, :, lanes], kt_out.at[tile, :, lanes]), (vt_s.at[tile, :, lanes], vt_out.at[tile, :, lanes])]
+
+    whole = [(cos_s, cos_out), (sin_s, sin_out), (posb_s, posb_out), (q_s, q_out), (k_s, k_out), (v_s, v_out),
+             (kt_s, kt_out), (vt_s, vt_out)]
+    n_rope = NBLK
+
+    def store(g, late):
+        for n, (src, dst) in enumerate(out_copies(g)):
+            if late == (n >= n_rope):
+                pltpu.make_async_copy(src, dst, osem.at[n]).start()
+
+    def products(blocks):
+        for g in blocks:
+            store_columns(full, nall, g, nall_sem)
+        rows = jnp.concatenate([full[g] for g in blocks], axis=0) if len(blocks) > ONE else full[blocks[0]]
+        for part in range(QKV // HD):
+            lin = dot(rows, w_s[:, head(part)])
+            for n, g in enumerate(blocks):
+                val = lin[BLK * n:BLK * n + BLK]
+                tile, lanes = lax.div(g * BLK, KT), lanes_at(lax.rem(g, KT // BLK), BLK)
+                if part < QW // HD:
+                    q_s[part, g] = (rope(val, cos_s[g], sin_s[g]) * q_scale).astype(BF16)
+                elif part == QW // HD:
+                    val = rope(val, cos_s[g], sin_s[g])
+                    k_s[g] = val.astype(BF16)
+                    kt_s[tile, :, lanes] = val.T.astype(BF16)
+                else:
+                    v_s[g] = val.astype(BF16)
+                    vt_s[tile, :, lanes] = val.T.astype(BF16)
+        for g in blocks:
+            store(g, True)
 
     @pl.loop(0, AG_STEPS)
     def _(s):
@@ -429,27 +496,19 @@
             angle = pos_b.astype(F32) * inv_freq[...]
             cos_s[g] = jnp.cos(angle)
             sin_s[g] = jnp.sin(angle)
-        pair = [ag_step(p, s, n, *ag) for n in range(TWO)]
-        ag_then(s, lambda way, i: ag_send(p, way, i, piece_of(full, p.me, i), *ag))
-        rows = jnp.concatenate([full[g] for g in pair], axis=0)
-        for part in range(QKV // HD):
-            lin = dot(rows, w_s[:, head(part)])
-            for n, g in enumerate(pair):
-                val = lin[BLK * n:BLK * n + BLK]
-                tile, lanes = lax.div(g * BLK, KT), lanes_at(lax.rem(g, KT // BLK), BLK)
-                if part < QW // HD:
-                    q_s[part, g] = (rope(val, cos_s[g], sin_s[g]) * q_scale).astype(BF16)
-                elif part == QW // HD:
-                    val = rope(val, cos_s[g], sin_s[g])
-                    k_s[g] = val.astype(BF16)
-                    kt_s[tile, :, lanes] = val.T.astype(BF16)
-                else:
-                    v_s[g] = val.astype(BF16)
-                    vt_s[tile, :, lanes] = val.T.astype(BF16)
-        for g in pair:
-            for n, (src, dst) in enumerate(out_copies(g)):
-                pltpu.make_async_copy(src, dst, osem.at[n]).start()
-            store_columns(full, nall, g, nall_sem)
+            store(g, False)
+
+        @pl.when(s == AG_LAST)
+        def _():
+            ag_last(p, *ag)
+            products([ag_block(p, s, 0)[-ONE]])
+            products([ag_step(p, s, ONE, *ag)])
+
+        @pl.when(s != AG_LAST)
+        def _():
+            pair = [ag_step(p, s, n, *ag) for n in range(TWO)]
+            ag_then(s, lambda way, i: ag_send(p, way, i, piece_of(full, p.me, i), *ag))
+            products(pair)
 
         @pl.when(s == CHIPS)
         def _():
@@ -472,21 +531,31 @@
 
 
 def attend_fwd_kernel(q, k, vt, posb, posr, wo, wop, x, gout, gain,
-                      o_out, ot_out, lse_out, y_out, dproj_out, dgain_out, *scratch):
+                      ot_out, lse_out, y_out, dproj_out, tail_out, dgain_out, *scratch):
     n_rs = len(rs_scratch(BLK))
     rs, rest = scratch[:n_rs], scratch[n_rs:]
     (q_s, k_s, vt_s, posb_s, wo_s, gain_s, x_s, go_s, o_s, ot_s, op_s, part, qt, s_buf, e_buf, l_buf, acc, yst, dgain, row_a,
-     row_b, lsem, op_ss, op_rs, osem, ysem) = rest
+     row_b, lsem, q_sem, op_ss, op_rs, osem, ysem, tail_sem) = rest
     fin, own = rs[HALF_PC], rs[HALF_PC + ONE]
     width = wo.shape[1]
     p = Place()
     loads = Loads(lsem)
-    first = [loads.add(q, q_s), loads.add(k, k_s), loads.add(posb, posb_s), loads.add(vt, vt_s)]
-    second = [loads.add(wo, wo_s.at[pl.ds(0, QW)]), loads.add(wop, wo_s.at[pl.ds(QW, QW)])]
-    third = [loads.add(x, x_s), loads.add(gout, go_s), loads.add(gain, gain_s.at[0])]
+
+    def q_load(s, flip):
+        chip = lax.rem(p.chip + RS_OFF[s], CHIPS)
+        g = (TWO * chip + lax.rem(p.core + flip, TWO)) * NBLK + RS_BLK[s]
+        return pltpu.make_async_copy(q.at[:, g], q_s.at[:, g], q_sem.at[flip, s])
+
+    first = [loads.add(k, k_s), loads.add(posb, posb_s), loads.add(vt, vt_s)]
+    for flip in range(TWO):
+        q_load(0, flip).start()
     e_buf[...] = jnp.zeros_like(e_buf)
     barrier((p.right, p.left, p.partner))
-    wait_all(first)
+    wait_all(first + [q_load(0, flip) for flip in range(TWO)])
+    second = [loads.add(wo, wo_s.at[pl.ds(0, QW)]), loads.add(wop, wo_s.at[pl.ds(QW, QW)])]
+    for s in range(ONE, RS_STEPS):
+        for flip in range(TWO):
+            q_load(s, flip).start()
 
     def attend(pair, swap):
         walk = Walk(*pair)
@@ -557,6 +626,7 @@
         @pl.when(s == 0)
         def _():
             wait_all(second)
+            wait_all([q_load(i, flip) for i in range(ONE, RS_STEPS) for flip in range(TWO)])
 
         swap.wait_recv()
         o_mine, o_part = o_s[mine], op_s[n]
@@ -568,82 +638,91 @@
 
         rs_emit(p, s, part, *rs)
 
-    outs = [pltpu.make_async_copy(o_s, o_out, osem.at[0]), pltpu.make_async_copy(ot_s, ot_out, osem.at[ONE])]
-    for copy in outs:
-        copy.start()
+    third = [loads.add(x, x_s), loads.add(gout, go_s), loads.add(gain, gain_s.at[0])]
+    outs = [pltpu.make_async_copy(ot_s, ot_out, osem)]
+    outs[0].start()
     wait_all(third)
     dgain[...] = jnp.zeros_like(dgain)
-    for blk in RS_DONE:
+    for blk in RS_DONE[:TWO]:
         rs_wait_block(p, blk, *rs)
-
-        @pl.loop(0, BLK // SUB)
-        def _(r, blk=blk):
-            rows, sums = rows16(r), []
-            for cols in column_groups(width):
-                val = rs_total(blk, r, cols, fin, own)
-                row_a[:, cols] = val
-                sums.append(fold(val * val))
-            inv = lax.rsqrt(row_mean(sums, width) + NORM_EPS)
-            sums = []
-            for cols in column_groups(width):
-                one_g = 1.0 + gain_s[:, cols]
-                go = go_s[blk, rows, cols].astype(F32)
-                nrm = row_a[:, cols] * inv
-                post = (nrm * one_g).astype(BF16).astype(F32)
-                yst[0, blk, rows, cols] = (x_s[blk, rows, cols].astype(F32) + post).astype(BF16)
-                dg = go * nrm
-                dgain[:, cols] += dg[:DEVS] + dg[DEVS:]
-                gog = go * one_g
-                row_a[:, cols] = nrm
-                row_b[:, cols] = gog
-                sums.append(fold(gog * nrm))
-            mean = row_mean(sums, width)
-            for cols in column_groups(width):
-                yst[ONE, blk, rows, cols] = (inv * (row_b[:, cols] - row_a[:, cols] * mean)).astype(BF16)
-
+        post_rows(functools.partial(rs_total, blk, fin, own), x_s.at[blk], go_s.at[blk], gain_s, yst.at[0, blk],
+                  yst.at[ONE, blk], dgain, row_a, row_b)
         for n, dst in enumerate((y_out, dproj_out)):
             copy = pltpu.make_async_copy(yst.at[n, blk], dst.at[blk], ysem.at[n, blk])
             copy.start()
             outs.append(copy)
     dgain_out[...] = jnp.sum(dgain[...], axis=0, keepdims=True)
+    blk = RS_DONE[TWO]
+    rs_wait_block(p, blk, *rs)
+    for h in range(TWO):
+        srcs = (own.at[blk, half_of(h), :], fin.at[0, TWO * blk + h], fin.at[ONE, TWO * blk + h])
+        for n, src in enumerate(srcs):
+            copy = pltpu.make_async_copy(src, tail_out.at[n, h], tail_sem.at[n, h])
+            copy.start()
+            outs.append(copy)
     for n in range(MY_BLK):
         rcopy(op_s.at[n], op_s.at[n], op_ss.at[n], op_rs.at[n], p.partner).wait_send()
     rs_finish(p, *rs)
     wait_all(outs)
 
 
-def attend_bwd_kernel(q_scale, dproj, wo, q, k, kt, v, o, lse, cos_t, sin_t, posb, posr,
-                      dall, dqkv_out, *scratch):
+def attend_bwd_kernel(q_scale, dproj, tail, x, gout, gain, dgain_in, wo, q, k, kt, v, ot, lse, cos_t, sin_t, posb, posr,
+                      dall, dqkv_out, y_out, dgain_out, *scratch):
     n_ag = len(ag_scratch(BLK))
     ag, rest = scratch[:n_ag], scratch[n_ag:]
-    (wo_s, q_s, k_s, kt_s, v_s, o_s, cos_s, sin_s, posb_s, dk_s, dv_s, dq_acc, out_s, qt, do_buf, dot_buf, delta, s_buf,
-     dp_buf, p_buf, ds_buf, lsem, osem, own_sem) = rest
+    (tail_s, x_s, go_s, gain_s, y_s, dgain, row_a, row_b, wo_s, q_s, k_s, kt_s, v_s, ot_s, cos_s, sin_s, posb_s, dk_s, dv_s, dq_acc, out_s, qt, do_buf, dot_buf, delta, s_buf,
+     dp_buf, p_buf, ds_buf, tail_sem, lsem, osem, own_sem, y_sem) = rest
     full = ag[0]
     p = Place()
+    last = RS_DONE[TWO]
+    early = Loads(tail_sem)
+    inputs = [early.add(src, dst) for src, dst in ((tail, tail_s), (x.at[last], x_s), (gout.at[last], go_s),
+                                                   (gain, gain_s.at[0]))]
+    barrier((p.right, p.left, p.partner))
+
+    def own_send(way, i):
+        src = dproj.at[i // TWO, half_of(i), :] if i // TWO != last else piece_of(full, p.me, i)
+        ag_send(p, way, i, src, *ag)
+
+    def own_sends(late):
+        for pieces in zip(*AG_FIRST):
+            for way, i in enumerate(pieces):
+                if (int(i) // TWO == last) == late:
+                    own_send(way, int(i))
+
+    own_sends(False)
+    own = [pltpu.make_async_copy(dproj.at[b], full.at[p.me * NBLK + b], own_sem.at[b]) for b in RS_DONE[:TWO]]
+    for b in RS_DONE[:TWO]:
+        ag_swap(p, p.chip, b, dproj.at[b], full.at[p.me * NBLK + b], *ag).start()
+    wait_all(inputs)
+    arrays = ((wo, wo_s), (ot, ot_s), (q, q_s), (k, k_s), (kt, kt_s), (v, v_s), (posb, posb_s), (cos_t, cos_s),
+              (sin_t, sin_s))
     loads = Loads(lsem)
-    barrier((p.right, p.left, p.partner))
-
-    def own_send(way, i):
-        ag_send(p, way, i, dproj.at[i // TWO, half_of(i), :], *ag)
-
-    for pieces in zip(*AG_FIRST):
-        for way, i in enumerate(pieces):
-            own_send(way, int(i))
-    for b in range(NBLK):
-        ag_swap(p, p.chip, b, dproj.at[b], full.at[p.me * NBLK + b], *ag).start()
-    own = pltpu.make_async_copy(dproj, full.at[pl.ds(p.me * NBLK, NBLK)], own_sem)
-    own.start()
-    for src, dst in ((wo, wo_s), (o, o_s), (q, q_s), (k, k_s), (kt, kt_s), (v, v_s), (posb, posb_s), (cos_t, cos_s),
-                     (sin_t, sin_s)):
-        loads.add(src, dst)
+    copies = [loads.add(src, dst) for src, dst in arrays]
+    for copy in own:
+        copy.start()
+    dgain[...] = jnp.zeros_like(dgain)
+
+    def tail_total(r, cols):
+        per = PIECE // SUB
+        h, rows = lax.div(r, per), rows16(lax.rem(r, per))
+        total = tail_s[0, h, rows, cols].astype(F32)
+        for n in (ONE, TWO):
+            total = total + tail_s[n, h, rows, cols].astype(F32)
+        return total.astype(BF16).astype(F32)
+
+    g_last = p.me * NBLK + last
+    post_rows(tail_total, x_s, go_s, gain_s, y_s, full.at[g_last], dgain, row_a, row_b)
+    own_sends(True)
+    ag_swap(p, p.chip, last, full.at[g_last], full.at[g_last], *ag).start()
+    y_copy = pltpu.make_async_copy(y_s, y_out.at[0], y_sem)
+    y_copy.start()
+    dgain_out[...] = dgain_in[...] + jnp.sum(dgain[...], axis=0, keepdims=True)
     dk_s[...] = jnp.zeros_like(dk_s)
     dv_s[...] = jnp.zeros_like(dv_s)
     p_buf[...] = jnp.zeros_like(p_buf)
     ds_buf[...] = jnp.zeros_like(ds_buf)
-    own.wait()
-    for n, (src, dst) in enumerate(((wo, wo_s), (o, o_s), (q, q_s), (k, k_s), (kt, kt_s), (v, v_s), (posb, posb_s),
-                                    (cos_t, cos_s), (sin_t, sin_s))):
-        pltpu.make_async_copy(src, dst, lsem.at[n]).wait()
+    wait_all(own + copies + [y_copy])
     dq_cols, kv_cols = pl.ds(0, QW), pl.ds(QW, QW)
 
     @pl.loop(0, AG_STEPS)
@@ -658,9 +737,11 @@
         for n, g in enumerate(pair):
             do2 = heads_down(do_all[BLK * n:BLK * n + BLK])
             do_buf[n] = do2
-            dot_buf[n] = do2.T
-            prod = do2.astype(F32) * heads_down(o_s[g]).astype(F32)
-            delta[n] = jnp.sum(prod.T, axis=0, keepdims=True)
+            do_t = do2.T
+            dot_buf[n] = do_t
+            lanes = lanes_at(g, BLK)
+            o_t = jnp.concatenate([ot_s[h, :, lanes] for h in range(TWO)], axis=1)
+            delta[n] = jnp.sum(do_t.astype(F32) * o_t.astype(F32), axis=0, keepdims=True)
             qt[n] = q_s[:, g].reshape(TWO * BLK, HD).T
         dq_acc[...] = jnp.zeros_like(dq_acc)
 
@@ -697,6 +778,10 @@
             scores(i + TWO, 0)
             products(i, 0)
             weights(i + ONE, ONE)
+
+            @pl.when(jnp.logical_and(s == AG_LAST - ONE, turn == jnp.minimum(TWO, walk.turns - ONE)))
+            def _():
+                ag_last(p, *ag)
 
         products(TWO * walk.turns - ONE, ONE)
         p_buf[...] = jnp.zeros_like(p_buf)
@@ -870,11 +955,12 @@
     copy.wait()
 
 
-def weight_grads_kernel(dqkv, nall, dall, ot, y, gq_out, gk_out, gv_out, gwo_out, y_out, *scratch):
+def weight_grads_kernel(dqkv, nall, dall, ot, y, y_last, gq_out, gk_out, gv_out, gwo_out, y_out, *scratch):
     d_s, in_s, gq_s, ot_s, gwo_s, y_s, lsem, isem, osem, wsem, ysem = scratch
     n_chunk = nall.shape[0]
     loads = Loads(lsem)
-    first, second = loads.add(ot, ot_s), loads.add(y, y_s)
+    first = loads.add(ot, ot_s)
+    second = [loads.add(y_last.at[0], y_s.at[RS_DONE[TWO]])] + [loads.add(y.at[b], y_s.at[b]) for b in RS_DONE[:TWO]]
     d_copy = loads.add(dqkv, d_s)
 
     ahead = in_s.shape[0] - ONE
@@ -927,7 +1013,7 @@
     first.wait()
     weight_grad(dall, 0, nall, wo_chunk, gwo_copies)
     d_copy.wait()
-    second.wait()
+    wait_all(second)
     y_copy = pltpu.make_async_copy(y_s, y_out, ysem)
     y_copy.start()
     weight_grad(nall, n_chunk, None, qkv_chunk, qkv_copies)
@@ -1103,29 +1189,32 @@
         tile_rows, tile_f = sds(k_t.shape, BF16), sds(k_t.shape, F32)
         tile_pos, score, square = sds(posb_t.shape, I32), sds((TWO, KT, HD), F32), sds((TWO, HD, HD), BF16)
         square_f, part = sds((TWO, HD, HD), F32), sds((BLK, width), F32)
-        o, ot, lse, y, dproj, dg_post = pl.pallas_call(
+        tail_all, row_block = sds((NBLK, TWO, PIECE, width), BF16), sds((BLK, width), BF16)
+        ot, lse, y, dproj, tail, dg_post = pl.pallas_call(
             attend_fwd_kernel, name='attend_fwd',
-            out_shape=(o_all, ot_all, lse_all, own_rows, own_rows, gain_row),
-            in_specs=specs('AAAAVAAAAA'), out_specs=specs('AAVAAV'),
+            out_shape=(ot_all, lse_all, own_rows, own_rows, tail_all, gain_row),
+            in_specs=specs('AAAAVAAAAA'), out_specs=specs('AVAAAV'),
             scratch_shapes=rs_scratch(width) + like(
                 q_all, tile_rows, tiles_t, tile_pos, w_t, gain_row, own_rows, own_rows, o_all, ot_all,
                 sds((MY_BLK, BLK, QW), BF16), part, square, score, sds(score.shape, BF16), sds((TWO, DEVS, HD), F32),
                 square_f, sds((TWO,) + x_blk.shape, BF16), sds((DEVS, width), F32), sds((SUB, width), F32),
                 sds((SUB, width), F32))
-            + [dma((9,)), dma((MY_BLK,)), dma((MY_BLK,)), dma((TWO,)), dma((TWO, NBLK))],
+            + [dma((8,)), dma((TWO, RS_STEPS)), dma((MY_BLK,)), dma((MY_BLK,)), dma(()), dma((TWO, NBLK)), dma((NBLK, TWO))],
             compiler_params=params(1),
         )(q, k_t, vt, posb_t, posr, wo, wop, x_blk, go_blk, gain_post)
 
-        dall, dqkv = pl.pallas_call(
+        dall, dqkv, y_last, dg_post = pl.pallas_call(
             functools.partial(attend_bwd_kernel, q_scale), name='attend_bwd',
-            out_shape=(all_bf, d_all),
-            in_specs=specs('AAAAAAAVAAAV'), out_specs=specs('AA'),
+            out_shape=(all_bf, d_all, sds((ONE, BLK, width), BF16), gain_row),
+            in_specs=specs('AAAAAVAAAAAAVAAAV'), out_specs=specs('AAAV'),
             scratch_shapes=ag_scratch(width) + like(
-                sds(wo.shape, BF16), q_all, tile_rows, tiles_t, tile_rows, o_all, rope_t, rope_t, tile_pos, tile_f, tile_f,
+                tail_all, row_block, row_block, gain_row, row_block, sds((DEVS, width), F32), sds((SUB, width), F32),
+                sds((SUB, width), F32), sds(wo.shape, BF16), q_all, tile_rows, tiles_t, tile_rows, ot_all, rope_t, rope_t, tile_pos, tile_f, tile_f,
                 square_f, d_all, square, square, square, sds((TWO, ONE, HD), F32), score, score, sds(score.shape, BF16),
-                sds(score.shape, BF16)) + [dma((9,)), dma((3,)), dma(())],
+                sds(score.shape, BF16))
+            + [dma((4,)), dma((9,)), dma((3,)), dma((NBLK,)), dma(())],
             compiler_params=params(2),
-        )(dproj, wo, q, k_t, kt, v_t, o, lse, cos_t, sin_t, posb_t, posr)
+        )(dproj, tail, x_blk, go_blk, gain_post, dg_post, wo, q, k_t, kt, v_t, ot, lse, cos_t, sin_t, posb_t, posr)
 
         hops = [sds((len(pieces), PIECE, width), BF16) for pieces in GROUPS]
         piece, own_pieces = sds((HALF_PC, PIECE, width), BF16), sds((NPC, PIECE, width), BF16)
@@ -1154,13 +1243,14 @@
             weight_grads_kernel, name='weight_grads',
             out_shape=(sds(w_query.shape, F32), sds(w_key.shape, F32), sds(w_value.shape, F32), sds(wo.shape, F32),
                        own_rows),
-            in_specs=specs('AAAAA'), out_specs=specs('AAAAA'),
+            in_specs=specs('AAAAAA'), out_specs=specs('AAAAA'),
             scratch_shapes=like(
                 d_all, sds((CHIPS, rows, HD), BF16), sds((TWO, HD, QKV), F32), sds((QW, rows), BF16), sds((TWO, QW, HD), F32),
-                own_rows) + [dma((3,)), dma((CHIPS,)), dma((TWO, CHIPS)), dma((TWO,)), dma(())],
+                own_rows) + [dma((5,)), dma((CHIPS,)), dma((TWO, CHIPS)), dma((TWO,)), dma(())],
             cost_estimate=pl.CostEstimate(flops=flops, bytes_accessed=TWO * rows * width * CHIPS, transcendentals=0),
             compiler_params=pltpu.CompilerParams(vmem_limit_bytes=VMEM_BYTES),
-        )(dqkv, *(a.reshape(width // HD, rows, HD) for a in (nall, dall)), ot.reshape(QW, rows), y)
+        )(dqkv, *(a.reshape(width // HD, rows, HD) for a in (nall, dall)), ot.reshape(QW, rows), y,
+          y_last)
         x_pc, go_pc = x_in.reshape(NPC, PIECE, width), grad_out.reshape(NPC, PIECE, width)
         gx, dgain = pre_grad(GROUPS[0], *hops_in[0], own, x_pc, go_pc, gain_pre)
         block = hops[ONE]

time: 448 us -> 434 us (0.969)
  waiting for transfers between devices: 11.5 us -> 1.4 us
  Pallas kernels: 428 us -> 423 us
    ppermute x4, waiting for transfers between devices: 11.5 us -> 1.4 us  [shift(): return lax.ppermute(rows_out, 'tp', ring)]
  transfers between devices with their start and end apart: 4 -> 4, of which waited for: 1 -> 1; matrix products, arithmetic and copies ran while one was open for 0% -> 0% of each run, Pallas kernels for 12% -> 13%
where the time goes in v2:
time: 434 us; the launch traced here: 432 us
  Pallas kernels  423 us (97%)
  starting transfers between devices  6.56 us (2%)
    pallas_call x1, Pallas kernels, local_step(): pl.pallas_call(functools.partial(attend_bwd_kernel, q_scale), name='atten...  110 us
    pallas_call x1, Pallas kernels, local_step(): pl.pallas_call(attend_fwd_kernel, name='attend_fwd', out_shape=(ot_all, l...  104 us
    pallas_call x1, Pallas kernels, local_step(): pl.pallas_call(functools.partial(gather_qkv_kernel, q_scale), name='gathe...  101 us
    pallas_call x1, Pallas kernels, local_step(): pl.pallas_call(weight_grads_kernel, name='weight_grads', out_shape=(sds(w...  44.9 us
    pallas_call x1, Pallas kernels, local_step(): pl.pallas_call(grad_rows_kernel, name='grad_rows', out_shape=hops + hops...  41.7 us
    pallas_call x1, Pallas kernels, pre_grad(): pl.pallas_call(functools.partial(pre_grad_kernel, pieces), name='pre_grad...  10.1 us
    pallas_call x1, Pallas kernels, local_step(): pl.pallas_call(last_rows_kernel, name='last_rows', out_shape=(block, sds(...  9.33 us
  transfers between devices with their start and end apart: 4, of which 1 were waited for; matrix products, arithmetic and copies ran while one was open for 0% of the time, Pallas kernels for 13%

profile of v2, /device:TPU:88, one launch (start us, length us, event | category | flops | bytes accessed | tf_op | source)
XLA Modules:
  0.0 432.3 jit_solution(13332062142080508797)
XLA Ops:
  0.6 100.6 %gather_qkv.1 = (bf16[14,24,128,256]{3,2,1,0:T(8,128)(2,1)}, bf16[2,24,128,256]{3,2,1,0:T(8,128)(2,1)}, bf16[24,128,256]{2,1,0:T(8,128)(2,1)}, bf16[24,128,256]{...) custom-call(bf16[3,128,3584]{2,1,0:T(8,128)(2,1)} %bitcast.17, ...), custom_call_target="tpu_custom_call" | custom-call | tf_op jit(solution)/shard_map/gather_qkv/pallas_call | solution.py:1177
  101.2 104.4 %attend_fwd.1 = (bf16[2,256,3072]{2,1,0:T(8,128)(2,1)}, f32[24,1,256]{2,1,0:T(1,128)}, bf16[3,128,3584]{2,1,0:T(8,128)(2,1)}, bf16[3,128,3584]{2,1,0:T(8,128)(2,...) custom-call(bf16[2,24,128,256]{3,2,1,0:T(8,128)(2,1)} %get-tuple-element.49.q, bf16[6,512,256]{2,1,0:T(8,128)(2,1)} %bitcast.29, ...), custom_call_target="tpu_custom_call" | custom-call | tf_op jit(solution)/shard_map/attend_fwd/pallas_call | solution.py:1193
  205.6 110.2 %attend_bwd.1 = (bf16[14,24,128,256]{3,2,1,0:T(8,128)(2,1)}, bf16[24,128,1024]{2,1,0:T(8,128)(2,1)}, bf16[1,128,3584]{2,1,0:T(8,128)(2,1)}, f32[1,3584]{1,0:T(1,128)}) custom-call(bf16[3,128,3584]{2,1,0:T(8,128)(2,1)} %get-tuple-element.55.dproj, bf16[3,2,64,3584]{3,2,1,0:T(8,128)(2,1)} %get-tuple-element.56.tail, bf16[3,128,3584]{2,1,0:T(8,128)(2,1)} %bitcast.19, ...), custom_call_target="tpu_custom_call" | custom-call | tf_op jit(solution)/shard_map/attend_bwd/pallas_call | solution.py:1206
  315.9 41.7 %grad_rows.1 = (bf16[4,64,3584]{2,1,0:T(8,128)(2,1)}, bf16[2,64,3584]{2,1,0:T(8,128)(2,1)}, bf16[4,64,3584]{2,1,0:T(8,128)(2,1)}, bf16[2,64,3584]{2,1,0:T(8,128)...) custom-call(bf16[24,128,1024]{2,1,0:T(8,128)(2,1)} %get-tuple-element.64.dqkv, ...), custom_call_target="tpu_custom_call" | custom-call | tf_op jit(solution)/shard_map/grad_rows/pallas_call | solution.py:1222
  357.6 0.1 collective-permute-start.2
  357.7 3.2 collective-permute-start.3
  360.9 0.0 collective-permute-start
  360.9 3.2 collective-permute-start.1
  364.1 44.9 %weight_grads.1 = (f32[3584,2,256]{2,1,0:T(2,128)}, f32[3584,1,256]{2,1,0:T(1,128)}, f32[3584,1,256]{2,1,0:T(1,128)}, f32[512,3584]{1,0:T(8,128)}, bf16[3,128,3584]{2,1,0:T(8,128)(2,1)}) custom-call(bf16[24,128,1024]{2,1,0:T(8,128)(2,1)} %get-tuple-element.64.dqkv, bf16[14,3072,256]{2,1,0:T(8,128)(2,1)} %bitcast.39, bf16[14,3072,256]{2,1,0:T(8,128)(2,1)} %bitcast.40, ...), custom_call_target="tpu_custom_call" | custom-call | flops 33822867456 | bytes 88080384 | tf_op jit(solution)/shard_map/weight_grads/pallas_call | solution.py:1242
  409.1 0.0 collective-permute-done.2.from_left
  409.1 0.0 collective-permute-done.3.from_right
  409.1 10.1 %pre_grad.1 = (bf16[6,64,3584]{2,1,0:T(8,128)(2,1)}, f32[8,3584]{1,0:T(8,128)}) custom-call(bf16[4,64,3584]{2,1,0:T(8,128)(2,1)} %collective-permute-done.2.from_left, bf16[4,64,3584]{2,1,0:T(8,128)(2,1)} %collective-permute-done.3.from_right, bf16[6,64,3584]{2,1,0:T(8,128)(2,1)} %get-tuple-element.75.own, bf16[6,64,3584]{2,1,0:T(8,128)(2,1)} %bitcast.20, ...), custom_call_target="tpu_custom_call" | custom-call | tf_op jit(solution)/shard_map/pre_grad/pallas_call | solution.py:1095
  419.2 1.4 collective-permute-done.from_left
  420.6 0.0 collective-permute-done.1.from_right
  420.6 9.3 %last_rows.1 = (bf16[2,64,3584]{2,1,0:T(8,128)(2,1)}, f32[3584]{0:T(1024)}) custom-call(bf16[2,64,3584]{2,1,0:T(8,128)(2,1)} %collective-permute-done.from_left, bf16[2,64,3584]{2,1,0:T(8,128)(2,1)} %collective-permute-done.1.from_right, bf16[6,64,3584]{2,1,0:T(8,128)(2,1)} %get-tuple-element.75.own, bf16[6,64,3584]{2,1,0:T(8,128)(2,1)} %bitcast.21, ...), custom_call_target="tpu_custom_call" | custom-call | tf_op jit(solution)/shard_map/last_rows/pallas_call | solution.py:1257
  429.9 2.2 finish.1
Async XLA Ops:
  357.6 51.5 %collective-permute-start.2 = (bf16[4,64,3584]{2,1,0:T(8,128)(2,1)}, bf16[4,64,3584]{2,1,0:T(8,128)(2,1)}, u32[]{:S(2)}, u32[]{:S(2)}) collective-permute-start(bf16[4,64,3584]{2,1,0:T(8,128)(2,1)} %get-tuple-element.76), channel_id=1, source_target_pairs={{0,2},{1,3},{2,4},{3,5},{4,6},{5,7},{6,0},{7,1},{8,10},{9,11},{10,... | collective-permute-start | bytes 5505032 | tf_op jit(solution)/shard_map/ppermute | solution.py:1236
  357.7 51.4 %collective-permute-start.3 = (bf16[4,64,3584]{2,1,0:T(8,128)(2,1)}, bf16[4,64,3584]{2,1,0:T(8,128)(2,1)}, u32[]{:S(2)}, u32[]{:S(2)}) collective-permute-start(bf16[4,64,3584]{2,1,0:T(8,128)(2,1)} %get-tuple-element.77), channel_id=1, source_target_pairs={{0,6},{1,7},{2,0},{3,1},{4,2},{5,3},{6,4},{7,5},{8,14},{9,15},{10,... | collective-permute-start | bytes 5505032 | tf_op jit(solution)/shard_map/ppermute | solution.py:1236
  360.9 59.7 %collective-permute-start = (bf16[2,64,3584]{2,1,0:T(8,128)(2,1)}, bf16[2,64,3584]{2,1,0:T(8,128)(2,1)}, u32[]{:S(2)}, u32[]{:S(2)}) collective-permute-start(bf16[2,64,3584]{2,1,0:T(8,128)(2,1)} %get-tuple-element.73), channel_id=1, source_target_pairs={{0,2},{1,3},{2,4},{3,5},{4,6},{5,7},{6,0},{7,1},{8,10},{9,11},{10,... | collective-permute-start | bytes 2752520 | tf_op jit(solution)/shard_map/ppermute | solution.py:1236
  360.9 59.7 %collective-permute-start.1 = (bf16[2,64,3584]{2,1,0:T(8,128)(2,1)}, bf16[2,64,3584]{2,1,0:T(8,128)(2,1)}, u32[]{:S(2)}, u32[]{:S(2)}) collective-permute-start(bf16[2,64,3584]{2,1,0:T(8,128)(2,1)} %get-tuple-element.74), channel_id=1, source_target_pairs={{0,6},{1,7},{2,0},{3,1},{4,2},{5,3},{6,4},{7,5},{8,14},{9,15},{10,... | collective-permute-start | bytes 2752520 | tf_op jit(solution)/shard_map/ppermute | solution.py:1236
